TPU v7x, 32 devices: a whole 2x2x4 slice. The times are simulated.
32 devices in a mesh: dp: 16 (over z, x, core), tensor: 2 (over y).
Axes of the slice: x: 2, y: 2, z: 4, core: 2. Of those that a mesh axis runs over, the one named last changes fastest.
Arguments:
- inputs: bfloat16 [16, 256, 4096], P('dp', 'tensor'), may hold values from -40 to 40
- query_states: bfloat16 [16, 256, 3072], P('dp', None, 'tensor'), may hold values from -4.5 to 4.5
- key_states: bfloat16 [16, 256, 1024], P('dp', None, 'tensor'), may hold values from -4.5 to 4.5
- saved_value_states: bfloat16 [16, 256, 1024], P('dp', None, 'tensor'), may hold values from -4.5 to 4.5
- head_cotangent: bfloat16 [16, 256, 3072], P('dp', None, 'tensor'), may hold values from -40 to 40
- query_weight: bfloat16 [4096, 3072], P('dp', 'tensor'), may hold values from -0.09375 to 0.09375
- key_matrix: bfloat16 [4096, 1024], P('dp', 'tensor'), may hold values from -0.09375 to 0.09375
- value_matrix: bfloat16 [4096, 1024], P('dp', 'tensor'), may hold values from -0.09375 to 0.09375
- query_momentum: float32 [4096, 3072], P('dp', 'tensor'), may hold values from -6 to 6
- key_prior_momentum: float32 [4096, 1024], P('dp', 'tensor'), may hold values from -6 to 6
- value_prior_momentum: float32 [4096, 1024], P('dp', 'tensor'), may hold values from -6 to 6
Outputs:
- input_gradient: bfloat16 [16, 256, 4096], P('dp', 'tensor')
- query_velocity: float32 [4096, 3072], P('dp', 'tensor')
- key_velocity: float32 [4096, 1024], P('dp', 'tensor')
- value_velocity: float32 [4096, 1024], P('dp', 'tensor')
All inputs are finite; a program needn't handle non-finite values.
Results may differ from a plain program's by a relative error of at most 0.019.
Values may be sent and summed in bfloat16 or wider, within the bound.
A program may use at most 128 MiB of HBM per device.

v0:
```python
import functools
import math

import jax
import jax.numpy as jnp
from jax import lax
from jax.experimental import pallas as pl
from jax.experimental.pallas import tpu as pltpu
from jax.sharding import PartitionSpec as P

HEAD_SIZE = 128
MESH = pl.DeviceIdType.MESH
F32 = jnp.float32
BF16 = jnp.bfloat16


def dot(a, b, ca, cb):
    return lax.dot_general(a, b, (((ca,), (cb,)), ((), ())), preferred_element_type=F32)


def kernel(
    nd, total_entries,
    x_ref, q_ref, k_ref, v_ref, do_ref, wq_ref, wk_ref, wv_ref,
    dx_ref, dwq_ref, dwk_ref, dwv_ref, fac_ref,
    g_all, x_all, w_cat, acc, p_buf, y_buf, d_buf, dxr, sqy, sq,
    xs_s, xs_r, xy_s, xy_r, ring_s, ring_r, dd_s, dd_r, py_s, py_r, dx_s, dx_r,
    sqy_s, sqy_r, sq_s, sq_r,
):
    kv = g_all.shape[1]
    seq = g_all.shape[2]
    wide = g_all.shape[3]
    grp = q_ref.shape[2] // k_ref.shape[2]
    gq = grp * HEAD_SIZE
    rows = wq_ref.shape[0]
    half = seq // 2
    nch = nd // 2
    d = lax.axis_index("dp")
    t = lax.axis_index("tensor")
    c = d % 2
    chip = d // 2
    xx = chip % 2
    zz = chip // 2
    pos = zz * (1 - xx) + (nch - 1 - zz) * xx
    dirn = 1 - 2 * c
    partner = chip * 2 + 1 - c

    def chip_of(p):
        p = (p + 2 * nch) % nch
        h = p // (nch // 2)
        z = p * (1 - h) + (nch - 1 - p) * h
        return 2 * z + h

    nxt = chip_of(pos + dirn) * 2 + c

    def ring_src(k):
        return chip_of(pos - dirn * (k + 1)) * 2 + c

    def partner_src(k):
        return chip_of(pos + dirn * (k + 1)) * 2 + 1 - c

    def to(dp, tt):
        return {"dp": dp, "tensor": tt}

    def rcopy(src, dst, ss, rs, dev):
        return pltpu.make_async_remote_copy(
            src_ref=src, dst_ref=dst, send_sem=ss, recv_sem=rs, device_id=dev, device_id_type=MESH
        )

    bar = pltpu.get_barrier_semaphore()

    def sig(i, _):
        pl.semaphore_signal(bar, inc=1, device_id=to((d + i) % nd, t), device_id_type=MESH)
        return 0

    lax.fori_loop(1, nd, sig, 0)
    pl.semaphore_signal(bar, inc=1, device_id=to(d, 1 - t), device_id_type=MESH)

    for j in range(kv):
        w_cat[j, :, 0:gq] = wq_ref[:, j * gq:(j + 1) * gq]
        w_cat[j, :, gq:gq + HEAD_SIZE] = wk_ref[:, j * HEAD_SIZE:(j + 1) * HEAD_SIZE]
        w_cat[j, :, gq + HEAD_SIZE:wide] = wv_ref[:, j * HEAD_SIZE:(j + 1) * HEAD_SIZE]
    acc[...] = jnp.zeros_like(acc)

    pl.semaphore_wait(bar, nd)

    def xcopy(e, slot):
        return rcopy(
            x_ref.at[0, :, pl.ds(pl.multiple_of(e * rows, 128), rows)],
            x_all.at[slot, t], xs_s.at[e], xs_r.at[slot], to(e, t),
        )

    def xsend(i, _):
        xcopy((d + i) % nd, d).start()
        return 0

    lax.fori_loop(1, nd, xsend, 0)
    x_all[d, t] = x_ref[0, :, pl.ds(pl.multiple_of(d * rows, 128), rows)]

    def xfwd(s):
        return rcopy(x_all.at[s, t], x_all.at[s, t], xy_s.at[s], xy_r.at[s], to(d, 1 - t))

    def xfwd_wait(s):
        rcopy(x_all.at[s, 1 - t], x_all.at[s, 1 - t], xy_s.at[s], xy_r.at[s], to(d, 1 - t)).wait_recv()

    xfwd(d).start()

    def ring(step, j, s):
        return rcopy(g_all.at[s, j], g_all.at[s, j], ring_s.at[step, j], ring_r.at[step, j], to(nxt, t))

    def d2d(step, j, s):
        return rcopy(g_all.at[s, j], g_all.at[s, j], dd_s.at[step, j], dd_r.at[step, j], to(partner, t))

    scaling = 1.0 / math.sqrt(HEAD_SIZE)

    def attention(j, _):
        kk = k_ref[0, :, pl.ds(pl.multiple_of(j * HEAD_SIZE, 128), HEAD_SIZE)]
        vv = v_ref[0, :, pl.ds(pl.multiple_of(j * HEAD_SIZE, 128), HEAD_SIZE)]
        dk = jnp.zeros((seq, HEAD_SIZE), F32)
        dv = jnp.zeros((seq, HEAD_SIZE), F32)
        mask = lax.broadcasted_iota(jnp.int32, (seq, seq), 0) >= lax.broadcasted_iota(
            jnp.int32, (seq, seq), 1
        )
        for g in range(grp):
            cols = pl.ds(pl.multiple_of(j * gq + g * HEAD_SIZE, 128), HEAD_SIZE)
            qq = q_ref[0, :, cols]
            oo = do_ref[0, :, cols]
            s = jnp.where(mask, dot(qq, kk, 1, 1) * scaling, -jnp.inf)
            e = jnp.exp(s - jnp.max(s, axis=-1, keepdims=True))
            soft = e / jnp.sum(e, axis=-1, keepdims=True)
            gs = dot(oo, vv, 1, 1)
            delta = jnp.sum(soft * gs, axis=-1, keepdims=True)
            ds = (soft * (gs - delta) * scaling).astype(BF16)
            g_all[d, j, :, g * HEAD_SIZE:(g + 1) * HEAD_SIZE] = dot(ds, kk, 1, 0).astype(BF16)
            dk = dk + dot(ds, qq, 0, 0)
            dv = dv + dot(soft.astype(BF16), oo, 0, 0)
        g_all[d, j, :, gq:gq + HEAD_SIZE] = dk.astype(BF16)
        g_all[d, j, :, gq + HEAD_SIZE:wide] = dv.astype(BF16)
        ring(0, j, d).start()
        d2d(0, j, d).start()
        return 0

    lax.fori_loop(0, kv, attention, 0)

    def xready(s):
        xcopy(s, s).wait_recv()
        xfwd(s).start()

    def pcopy(s):
        return rcopy(p_buf.at[s, 1 - t], y_buf.at[s], py_s.at[s], py_r.at[s], to(d, 1 - t))

    def block(s):
        xfwd_wait(s)
        xb = x_all[s].reshape(seq, rows)
        part = jnp.zeros((seq, rows), F32)
        for j in range(kv):
            gb = g_all[s, j]
            part = part + dot(gb, w_cat[j], 1, 1)
            acc[j] += dot(xb, gb, 0, 0)
        p_buf[s] = part.astype(BF16).reshape(2, half, rows)
        pcopy(s).start()

    def reduced(s):
        pcopy(s).wait_recv()
        return (p_buf[s, t].astype(F32) + y_buf[s].astype(F32)).astype(BF16)

    def dxcopy(s, slot):
        return rcopy(d_buf.at[s], dxr.at[slot], dx_s.at[s], dx_r.at[slot], to(s, t))

    def finish(s):
        d_buf[s] = reduced(s)
        dxcopy(s, d).start()

    xready(partner)
    block(d)
    for j in range(kv):
        d2d(0, j, partner).wait_recv()
    block(partner)
    dxr[d] = reduced(d)
    steps = nch - 1

    def step(k, _):
        sa = ring_src(k)
        sb = partner_src(k)
        xready(sa)
        xready(sb)
        for j in range(kv):
            ring(k, j, sa).wait_recv()

            @pl.when(k < steps - 1)
            def _():
                ring(k + 1, j, sa).start()

            d2d(k + 1, j, sa).start()
        block(sa)
        for j in range(kv):
            d2d(k + 1, j, sb).wait_recv()
        block(sb)

        @pl.when(k == 0)
        def _():
            finish(partner)

        @pl.when(k > 0)
        def _():
            finish(ring_src(k - 1))
            finish(partner_src(k - 1))

        return 0

    lax.fori_loop(0, steps, step, 0)

    squares = jnp.zeros((1, 1), F32)
    for j in range(kv):
        a = acc[j]
        squares = squares + jnp.sum(a * a, keepdims=True)
    sqy[t] = jnp.broadcast_to(squares, (8, 128))
    sqc = rcopy(sqy.at[t], sqy.at[t], sqy_s, sqy_r, to(d, 1 - t))
    sqc.start()
    finish(ring_src(steps - 1))
    finish(partner_src(steps - 1))
    rcopy(sqy.at[1 - t], sqy.at[1 - t], sqy_s, sqy_r, to(d, 1 - t)).wait_recv()
    sq[d] = sqy[0] + sqy[1]

    def sqcopy(e, slot):
        return rcopy(sq.at[slot], sq.at[slot], sq_s.at[e], sq_r.at[slot], to(e, t))

    def sqsend(i, _):
        sqcopy((d + i) % nd, d).start()
        return 0

    lax.fori_loop(1, nd, sqsend, 0)
    for j in range(kv):
        dwq_ref[:, j * gq:(j + 1) * gq] = acc[j, :, 0:gq]
        dwk_ref[:, j * HEAD_SIZE:(j + 1) * HEAD_SIZE] = acc[j, :, gq:gq + HEAD_SIZE]
        dwv_ref[:, j * HEAD_SIZE:(j + 1) * HEAD_SIZE] = acc[j, :, gq + HEAD_SIZE:wide]

    def drain(i, _):
        e = (d + i) % nd
        xcopy(e, d).wait_send()
        dxcopy(e, d).wait_send()
        dxcopy(e, e).wait_recv()
        sqcopy(e, d).wait_send()
        sqcopy(e, e).wait_recv()
        return 0

    lax.fori_loop(1, nd, drain, 0)

    def drain_all(s, _):
        xfwd(s).wait_send()
        pcopy(s).wait_send()
        return 0

    lax.fori_loop(0, nd, drain_all, 0)
    sqc.wait_send()
    for j in range(kv):
        def drain_g(k, _):
            ring(k, j, d).wait_send()
            d2d(k, j, d).wait_send()
            return 0

        lax.fori_loop(0, steps, drain_g, 0)
        d2d(steps, j, d).wait_send()
    for e in range(nd):
        dx_ref[0, :, e * rows:(e + 1) * rows] = dxr[e]
    total = jnp.sum(sq[...], axis=0)
    fac_ref[...] = 1.0 / jnp.maximum(jnp.sqrt(total / total_entries), 1.0)


def fused(nd, nt, inputs, q, k, v, do, wq, wk, wv):
    seq = q.shape[1]
    kv = k.shape[2] // HEAD_SIZE
    wide = (q.shape[2] + 2 * k.shape[2]) // kv
    rows = wq.shape[0]
    half = seq // nt
    total_entries = float(rows * nd * kv * wide * nt)
    vm = pl.BlockSpec(memory_space=pltpu.VMEM)
    dma = pltpu.SemaphoreType.DMA
    steps = nd // 2 - 1
    return pl.pallas_call(
        functools.partial(kernel, nd, total_entries),
        out_shape=(
            jax.ShapeDtypeStruct(inputs.shape, BF16),
            jax.ShapeDtypeStruct(wq.shape, F32),
            jax.ShapeDtypeStruct(wk.shape, F32),
            jax.ShapeDtypeStruct(wv.shape, F32),
            jax.ShapeDtypeStruct((8, 128), F32),
        ),
        in_specs=[vm] * 8,
        out_specs=(vm,) * 5,
        scratch_shapes=[
            pltpu.VMEM((nd, kv, seq, wide), BF16),
            pltpu.VMEM((nd, nt, half, rows), BF16),
            pltpu.VMEM((kv, rows, wide), BF16),
            pltpu.VMEM((kv, rows, wide), F32),
            pltpu.VMEM((nd, nt, half, rows), BF16),
            pltpu.VMEM((nd, half, rows), BF16),
            pltpu.VMEM((nd, half, rows), BF16),
            pltpu.VMEM((nd, half, rows), BF16),
            pltpu.VMEM((2, 8, 128), F32),
            pltpu.VMEM((nd, 8, 128), F32),
            dma((nd,)), dma((nd,)), dma((nd,)), dma((nd,)),
            dma((steps, kv)), dma((steps, kv)), dma((steps + 1, kv)), dma((steps + 1, kv)),
            dma((nd,)), dma((nd,)), dma((nd,)), dma((nd,)),
            dma, dma, dma((nd,)), dma((nd,)),
        ],
        compiler_params=pltpu.CompilerParams(
            collective_id=0, has_side_effects=True, vmem_limit_bytes=60 * 1024 * 1024
        ),
    )(inputs, q, k, v, do, wq, wk, wv)


def heads_backward(query_row_set, key_rows, value_rows, cotangent_rows):
    token_length = query_row_set.shape[0]
    kv_heads = key_rows.shape[1] // HEAD_SIZE
    group_width = query_row_set.shape[1] // HEAD_SIZE // kv_heads
    scaling = 1.0 / math.sqrt(HEAD_SIZE)
    query_quad = query_row_set.reshape(token_length, kv_heads, group_width, HEAD_SIZE)
    cotangent_quad = cotangent_rows.reshape(token_length, kv_heads, group_width, HEAD_SIZE)
    key_triple = key_rows.reshape(token_length, kv_heads, HEAD_SIZE)
    value_triple = value_rows.reshape(token_length, kv_heads, HEAD_SIZE)
    block_rows = min(token_length, 512)
    key_sums = jnp.zeros((token_length, kv_heads, HEAD_SIZE), F32)
    value_sums = jnp.zeros((token_length, kv_heads, HEAD_SIZE), F32)
    query_blocks = []
    for row_start in range(0, token_length, block_rows):
        row_end = row_start + block_rows
        query_block = query_quad[row_start:row_end]
        cotangent_block = cotangent_quad[row_start:row_end]
        key_block = key_triple[:row_end]
        value_block = value_triple[:row_end]
        scores = (
            jnp.einsum("ihgd,jhd->hgij", query_block, key_block, preferred_element_type=F32)
            * scaling
        )
        query_index = row_start + lax.broadcasted_iota(jnp.int32, (block_rows, row_end), 0)
        key_index = lax.broadcasted_iota(jnp.int32, (block_rows, row_end), 1)
        scores = jnp.where(query_index >= key_index, scores, -jnp.inf)
        maximum = jnp.max(scores, axis=-1, keepdims=True)
        exponent = jnp.exp(scores - maximum)
        softmax_rows = exponent / jnp.sum(exponent, axis=-1, keepdims=True)
        softmax_reduced = softmax_rows.astype(BF16)
        grad_softmax = jnp.einsum(
            "ihgd,jhd->hgij", cotangent_block, value_block, preferred_element_type=F32
        )
        row_delta = jnp.sum(softmax_rows * grad_softmax, axis=-1, keepdims=True)
        score_gradient = (softmax_rows * (grad_softmax - row_delta) * scaling).astype(BF16)
        query_blocks.append(
            jnp.einsum(
                "hgij,jhd->ihgd", score_gradient, key_block, preferred_element_type=F32
            ).astype(BF16)
        )
        key_sums = key_sums.at[:row_end].add(
            jnp.einsum(
                "xfwo,wxfp->oxp", score_gradient, query_block, preferred_element_type=F32
            )
        )
        value_sums = value_sums.at[:row_end].add(
            jnp.einsum(
                "xfwo,wxfp->oxp",
                softmax_reduced,
                cotangent_block,
                preferred_element_type=F32,
            )
        )
    grad_query = jnp.concatenate(query_blocks, axis=0).reshape(token_length, -1)
    key_gradient = key_sums.astype(BF16).reshape(token_length, -1)
    value_gradient = value_sums.astype(BF16).reshape(token_length, -1)
    return (grad_query, key_gradient, value_gradient)


def small(nd, nt, inputs, query_states, key_states, query_weight):
    seq = query_states.shape[1]
    cols = query_states.shape[2] + 2 * key_states.shape[2]
    held = nd * seq * cols * 2 + 10 * nd * seq * query_weight.shape[0]
    return nt == 2 and nd % 4 == 0 and nd >= 8 and held < 36 * 1024 * 1024


def local(nd, nt, *args):
    inputs, q, k, v, do, wq, wk, wv, mq, mk, mv = args
    if small(nd, nt, inputs, q, k, wq):
        grad_inputs, gq, gk, gv, fac = fused(nd, nt, inputs, q, k, v, do, wq, wk, wv)
        factor = fac[0, 0]
    else:
        query_cols = wq.shape[1]
        pair_cols = wk.shape[1]
        rows = wq.shape[0]
        weights = jnp.concatenate((wq, wk, wv), axis=1)
        grads = jnp.concatenate(heads_backward(q[0], k[0], v[0], do[0]), axis=1)
        all_grads = lax.all_gather(grads, "dp", axis=0, tiled=True)
        pieces = lax.all_to_all(inputs[0], "dp", 1, 0, tiled=True)
        pieces = pieces.reshape(nd, -1, rows)
        all_inputs = lax.all_gather(pieces, "tensor", axis=1, tiled=True).reshape(-1, rows)
        summed = dot(all_inputs, all_grads, 0, 0)
        parts = dot(all_grads, weights, 1, 1).astype(BF16).reshape(nd, -1, rows)
        mine = lax.psum_scatter(parts, "tensor", scatter_dimension=1, tiled=True)
        grad_inputs = lax.all_to_all(mine.reshape(-1, rows), "dp", 0, 1, tiled=True)[None]
        total = lax.psum(jnp.sum(summed * summed), ("dp", "tensor"))
        factor = 1.0 / jnp.maximum(jnp.sqrt(total / (summed.size * nd * nt)), 1.0)
        gq = summed[:, :query_cols]
        gk = summed[:, query_cols:query_cols + pair_cols]
        gv = summed[:, query_cols + pair_cols:]
    return (
        grad_inputs,
        0.9 * mq + factor * gq,
        0.9 * mk + factor * gk,
        0.9 * mv + factor * gv,
    )


def solution(mesh):
    nd, nt = mesh.shape["dp"], mesh.shape["tensor"]
    saved = P("dp", None, "tensor")
    tokens = P("dp", "tensor", None)
    weight = P("dp", "tensor")
    return jax.shard_map(
        functools.partial(local, nd, nt),
        mesh=mesh,
        in_specs=(tokens,) + (saved,) * 4 + (weight,) * 6,
        out_specs=(tokens,) + (weight,) * 3,
        check_vma=False,
    )
```

profile of v0, /device:TPU:0, one launch (start us, length us, event | category | flops | bytes accessed | tf_op | source)
XLA Modules:
  0.0 174.2 jit_solution(10928261799036791986)
XLA Ops:
  0.6 0.0 copy-start.3
  0.6 0.0 copy-start.4
  0.7 165.9 %shard_map.138 = (bf16[1,128,4096]{2,1,0:T(8,128)(2,1)}, f32[256,1536]{1,0:T(8,128)}, f32[256,512]{1,0:T(8,128)}, f32[256,512]{1,0:T(8,128)}, f32[8,128]{1,0:T(8,128)}) custom-call(bf16[1,128,4096]{2,1,0:T(8,128)(2,1)} %x_ref.1, bf16[1,256,1536]{2,1,0:T(8,128)(2,1)} %q_ref.1, bf16[1,256,512]{2,1,0:T(8,128)(2,1)} %k_ref.1, bf16[1,256,512]{2,1,0:T(8,128)(2,1)} %v_ref.1, ...), custom_call_target="tpu_custom_call" | custom-call | tf_op jit(solution)/shard_map/pallas_call | solution.py:279
  166.6 1.2 slice.3
  167.7 0.0 copy-done.3
  167.7 0.0 copy-done.4
  167.7 0.0 copy-start
  167.8 0.0 copy-start.1
  167.8 3.4 %multiply_add_fusion.1 = (f32[256,512]{1,0:T(8,128)}, f32[256,512]{1,0:T(8,128)}) fusion(f32[256,512]{1,0:T(8,128)} %get-tuple-element.13, f32[256,512]{1,0:T(8,128)S(1)} %copy-done.3, f32[]{:T(128)} %bitcast, f32[256,512]{1,0:T(8,128)} %get-tuple-element.12, f32[256,512]{1,0:T(8,128)S(1)} %copy-done.4), kind=kLoop, calls=%fused_computation.1 | loop fusion | flops 786432 | bytes 3145732 | tf_op jit(solution)/shard_map/add | solution.py:406
  171.1 0.0 copy-done
  171.1 0.0 copy-done.1
  171.1 0.0 copy-start.2
  171.1 2.1 %multiply_add_fusion = f32[256,1536]{1,0:T(8,128)} fusion(f32[256,1536]{1,0:T(8,128)S(1)} %copy-done.1, f32[256,1536]{1,0:T(8,128)S(1)} %copy-done, f32[]{:T(128)} %bitcast), kind=kLoop, calls=%fused_computation | loop fusion | flops 1179648 | bytes 4718596 | tf_op jit(solution)/shard_map/add | solution.py:404
  173.3 0.0 copy-done.2
  173.3 1.0 copy.16
Async XLA Ops:
  0.6 167.1 %copy-start.3 = (f32[256,512]{1,0:T(8,128)S(1)}, f32[256,512]{1,0:T(8,128)}, u32[]{:S(2)}) copy-start(f32[256,512]{1,0:T(8,128)} %param.21) | copy-start | bytes 1572868
  0.6 167.1 %copy-start.4 = (f32[256,512]{1,0:T(8,128)S(1)}, f32[256,512]{1,0:T(8,128)}, u32[]{:S(2)}) copy-start(f32[256,512]{1,0:T(8,128)} %param.20) | copy-start | bytes 1572868
  167.7 3.4 %copy-start = (f32[256,1536]{1,0:T(8,128)S(1)}, f32[256,1536]{1,0:T(8,128)}, u32[]{:S(2)}) copy-start(f32[256,1536]{1,0:T(8,128)} %param.19) | copy-start | bytes 4718596
  167.8 3.4 %copy-start.1 = (f32[256,1536]{1,0:T(8,128)S(1)}, f32[256,1536]{1,0:T(8,128)}, u32[]{:S(2)}) copy-start(f32[256,1536]{1,0:T(8,128)} %get-tuple-element.11) | copy-start | bytes 4718596
  171.1 2.2 %copy-start.2 = (bf16[1,128,4096]{2,1,0:T(8,128)(2,1)S(1)}, bf16[1,128,4096]{2,1,0:T(8,128)(2,1)}, u32[]{:S(2)}) copy-start(bf16[1,128,4096]{2,1,0:T(8,128)(2,1)} %get-tuple-element.20) | copy-start | bytes 3145732
where the time goes:
time: 174 us
  Pallas kernels  166 us (95%)
  other arithmetic  5.5 us (3%)
  local copies, waits for them, and re-layouts  2.18 us (1%)
    pallas_call x1, Pallas kernels, fused(): pl.pallas_call(functools.partial(kernel, nd, total_entries), out_shape=(j...  166 us

commit v1 on v0

v1 whole, which is shorter than its diff:
```python
import functools
import math

import jax
import jax.numpy as jnp
from jax import lax
from jax.experimental import pallas as pl
from jax.experimental.pallas import tpu as pltpu
from jax.sharding import PartitionSpec as P

HEAD_SIZE = 128
MESH = pl.DeviceIdType.MESH
F32 = jnp.float32
BF16 = jnp.bfloat16
W_FIRST = 1


def dot(a, b, ca, cb):
    return lax.dot_general(a, b, (((ca,), (cb,)), ((), ())), preferred_element_type=F32)


def kernel(
    nd, total_entries,
    x_ref, q_ref, k_ref, v_ref, do_ref, wq_ref, wk_ref, wv_ref,
    dx_ref, dwq_ref, dwk_ref, dwv_ref, fac_ref,
    g_all, x_all, w_cat, acc, part, p_buf, y_buf, d_buf, ws, wr, sq,
    xs_s, xs_r, xy_s, xy_r, w_s, w_r, col_s, col_r, xn_s, xn_r, dd_s, dd_r,
    py_s, py_r, dx_s, dx_r, dw_s, dw_r, sq_s, sq_r,
):
    kv = g_all.shape[0]
    group = g_all.shape[1]
    seq = g_all.shape[2]
    wide = g_all.shape[3]
    grp = q_ref.shape[2] // k_ref.shape[2]
    gq = grp * HEAD_SIZE
    rows = wq_ref.shape[0]
    half = seq // 2
    near = group // 2
    nz = nd // 4
    d = lax.axis_index("dp")
    t = lax.axis_index("tensor")
    c = d % 2
    xx = (d // 2) % 2
    z = d // 4

    def other_half(e):
        return e + 4 * (1 - 2 * ((e // 4) % 2))

    def member(r):
        zr = nz - 1 - z if r & 4 else z
        xr = 1 - xx if r & 2 else xx
        cr = 1 - c if r & 1 else c
        return (zr * 2 + xr) * 2 + cr

    def columns(e):
        return pl.ds(pl.multiple_of(e * rows, 128), rows)

    def to(dp, tt):
        return {"dp": dp, "tensor": tt}

    def rcopy(src, dst, ss, rs, dev):
        return pltpu.make_async_remote_copy(
            src_ref=src, dst_ref=dst, send_sem=ss, recv_sem=rs, device_id=dev, device_id_type=MESH
        )

    far = other_half(d)
    me = d * 2 + t
    total_devices = nd * 2
    bar = pltpu.get_barrier_semaphore()

    def sig(i, _):
        e = (me + i) % total_devices
        pl.semaphore_signal(bar, inc=1, device_id=to(e // 2, e % 2), device_id_type=MESH)
        return 0

    lax.fori_loop(1, total_devices, sig, 0)

    for j in range(kv):
        w_cat[j, 0:rows, 0:gq] = wq_ref[:, j * gq:(j + 1) * gq]
        w_cat[j, 0:rows, gq:gq + HEAD_SIZE] = wk_ref[:, j * HEAD_SIZE:(j + 1) * HEAD_SIZE]
        w_cat[j, 0:rows, gq + HEAD_SIZE:wide] = wv_ref[:, j * HEAD_SIZE:(j + 1) * HEAD_SIZE]

    pl.semaphore_wait(bar, total_devices - 1)

    def xcopy(r, f):
        e = member(r)
        src = e if f == 0 else other_half(e)
        return rcopy(
            x_ref.at[0, :, columns(src)], x_all.at[r, t, :, f * rows:(f + 1) * rows],
            xs_s.at[r, f], xs_r.at[r, f], to(e, t),
        )

    def xfwd(r):
        return rcopy(x_all.at[r, t], x_all.at[r, t], xy_s.at[r], xy_r.at[r], to(d, 1 - t))

    def xfwd_wait(r):
        rcopy(x_all.at[r, 1 - t], x_all.at[r, 1 - t], xy_s.at[r], xy_r.at[r], to(d, 1 - t)).wait_recv()

    def wcopy(j):
        return rcopy(
            w_cat.at[j, 0:rows], w_cat.at[j, rows:2 * rows], w_s.at[j], w_r.at[j], to(far, t)
        )

    def colcopy(j):
        return rcopy(g_all.at[j, 0], g_all.at[j, 4], col_s.at[j], col_r.at[j], to(member(4), t))

    def xncopy(i, j):
        return rcopy(
            g_all.at[j, 4 * i], g_all.at[j, 4 * i + 2], xn_s.at[i, j], xn_r.at[i, j], to(member(2), t)
        )

    def ddcopy(i, j):
        return rcopy(
            g_all.at[j, 2 * i], g_all.at[j, 2 * i + 1], dd_s.at[i, j], dd_r.at[i, j], to(member(1), t)
        )

    for r in (4, 5, 6, 7, 2, 3, 1):
        for f in range(2):
            xcopy(r, f).start()
    for f, e in ((0, d), (1, far)):
        x_all[0, t, :, f * rows:(f + 1) * rows] = x_ref[0, :, columns(e)]
    xfwd(0).start()
    for j in range(W_FIRST):
        wcopy(j).start()

    scaling = 1.0 / math.sqrt(HEAD_SIZE)

    def attention(j, _):
        kk = k_ref[0, :, pl.ds(pl.multiple_of(j * HEAD_SIZE, 128), HEAD_SIZE)]
        vv = v_ref[0, :, pl.ds(pl.multiple_of(j * HEAD_SIZE, 128), HEAD_SIZE)]
        dk = jnp.zeros((seq, HEAD_SIZE), F32)
        dv = jnp.zeros((seq, HEAD_SIZE), F32)
        mask = lax.broadcasted_iota(jnp.int32, (seq, seq), 0) >= lax.broadcasted_iota(
            jnp.int32, (seq, seq), 1
        )
        for g in range(grp):
            cols = pl.ds(pl.multiple_of(j * gq + g * HEAD_SIZE, 128), HEAD_SIZE)
            qq = q_ref[0, :, cols]
            oo = do_ref[0, :, cols]
            s = jnp.where(mask, dot(qq, kk, 1, 1) * scaling, -jnp.inf)
            e = jnp.exp(s - jnp.max(s, axis=-1, keepdims=True))
            soft = e / jnp.sum(e, axis=-1, keepdims=True)
            gs = dot(oo, vv, 1, 1)
            delta = jnp.sum(soft * gs, axis=-1, keepdims=True)
            ds = (soft * (gs - delta) * scaling).astype(BF16)
            g_all[j, 0, :, g * HEAD_SIZE:(g + 1) * HEAD_SIZE] = dot(ds, kk, 1, 0).astype(BF16)
            dk = dk + dot(ds, qq, 0, 0)
            dv = dv + dot(soft.astype(BF16), oo, 0, 0)
        g_all[j, 0, :, gq:gq + HEAD_SIZE] = dk.astype(BF16)
        g_all[j, 0, :, gq + HEAD_SIZE:wide] = dv.astype(BF16)
        colcopy(j).start()
        xncopy(0, j).start()
        ddcopy(0, j).start()
        return 0

    lax.fori_loop(0, kv, attention, 0)
    for j in range(W_FIRST, kv):
        wcopy(j).start()

    def xready(r):
        for f in range(2):
            xcopy(r, f).wait_recv()
        xfwd(r).start()

    for r in range(1, group):
        xready(r)

    def neighbours(j, _):
        xncopy(0, j).wait_recv()
        ddcopy(1, j).start()
        ddcopy(0, j).wait_recv()
        return 0

    lax.fori_loop(0, kv, neighbours, 0)
    for r in range(group):
        xfwd_wait(r)

    def near_weights(j, _):
        ddcopy(1, j).wait_recv()
        acc[j] = dot(x_all[0:near].reshape(near * seq, 2 * rows), g_all[j, 0:near].reshape(near * seq, wide), 0, 0)
        return 0

    lax.fori_loop(0, kv, near_weights, 0)

    def partial(j, lo):
        gs = g_all[j, lo:lo + near].reshape(near * seq, wide)
        return dot(gs, w_cat[j], 1, 1)

    def near_inputs(j, _):
        wcopy(j).wait_recv()

        @pl.when(j == 0)
        def _():
            part[...] = partial(j, 0)

        @pl.when(j > 0)
        def _():
            part[...] += partial(j, 0)

        return 0

    lax.fori_loop(0, kv, near_inputs, 0)

    def pcopy(r):
        return rcopy(p_buf.at[r, 1 - t], y_buf.at[r], py_s.at[r], py_r.at[r], to(d, 1 - t))

    def exchange(lo):
        for r in range(near):
            p_buf[lo + r] = part[r * seq:(r + 1) * seq].astype(BF16).reshape(2, half, 2 * rows)
            pcopy(lo + r).start()

    exchange(0)

    def dxcopy(r, f):
        e = d if f == 0 else far
        return rcopy(
            d_buf.at[r, :, f * rows:(f + 1) * rows], dx_ref.at[0, :, columns(e)],
            dx_s.at[r, f], dx_r.at[r, f], to(member(r), t),
        )

    def dxwait(r, f):
        e = member(r)
        e = e if f == 0 else other_half(e)
        rcopy(
            d_buf.at[r, :, f * rows:(f + 1) * rows], dx_ref.at[0, :, columns(e)],
            dx_s.at[r, f], dx_r.at[r, f], to(member(r), t),
        ).wait_recv()

    def finish(r):
        pcopy(r).wait_recv()
        total = (p_buf[r, t].astype(F32) + y_buf[r].astype(F32)).astype(BF16)
        if r == 0:
            for f, e in ((0, d), (1, far)):
                dx_ref[0, :, columns(e)] = total[:, f * rows:(f + 1) * rows]
        else:
            d_buf[r] = total
            for f in range(2):
                dxcopy(r, f).start()

    def dwcopy(j):
        return rcopy(ws.at[j], wr.at[j], dw_s.at[j], dw_r.at[j], to(far, t))

    def distant(j, _):
        colcopy(j).wait_recv()
        xncopy(1, j).start()
        ddcopy(2, j).start()

        @pl.when(j == 0)
        def _():
            for r in range(near):
                finish(r)

        xncopy(1, j).wait_recv()
        ddcopy(3, j).start()
        ddcopy(2, j).wait_recv()
        ddcopy(3, j).wait_recv()
        acc[j] += dot(
            x_all[near:group].reshape(near * seq, 2 * rows),
            g_all[j, near:group].reshape(near * seq, wide), 0, 0,
        )
        ws[j] = acc[j, rows:2 * rows].astype(BF16)
        dwcopy(j).start()

        @pl.when(j == 0)
        def _():
            part[...] = partial(j, near)

        @pl.when(j > 0)
        def _():
            part[...] += partial(j, near)

        return 0

    lax.fori_loop(0, kv, distant, 0)
    exchange(near)
    for r in range(near, group):
        finish(r)

    squares = jnp.zeros((1, 1), F32)
    for j in range(kv):
        dwcopy(j).wait_recv()
        a = acc[j, 0:rows] + wr[j].astype(F32)
        acc[j, 0:rows] = a
        squares = squares + jnp.sum(a * a, keepdims=True)
    sq[me] = jnp.broadcast_to(squares, (8, 128))

    def sqcopy(e, slot):
        return rcopy(sq.at[slot], sq.at[slot], sq_s.at[e], sq_r.at[slot], to(e // 2, e % 2))

    def sqsend(i, _):
        sqcopy((me + i) % total_devices, me).start()
        return 0

    lax.fori_loop(1, total_devices, sqsend, 0)
    for j in range(kv):
        dwq_ref[:, j * gq:(j + 1) * gq] = acc[j, 0:rows, 0:gq]
        dwk_ref[:, j * HEAD_SIZE:(j + 1) * HEAD_SIZE] = acc[j, 0:rows, gq:gq + HEAD_SIZE]
        dwv_ref[:, j * HEAD_SIZE:(j + 1) * HEAD_SIZE] = acc[j, 0:rows, gq + HEAD_SIZE:wide]

    for r in range(1, group):
        for f in range(2):
            xcopy(r, f).wait_send()
            dxcopy(r, f).wait_send()
            dxwait(r, f)
    for r in range(group):
        xfwd(r).wait_send()
        pcopy(r).wait_send()

    def drain_g(j, _):
        wcopy(j).wait_send()
        dwcopy(j).wait_send()
        colcopy(j).wait_send()
        for i in range(2):
            xncopy(i, j).wait_send()
        for i in range(4):
            ddcopy(i, j).wait_send()
        return 0

    lax.fori_loop(0, kv, drain_g, 0)

    def drain(i, _):
        e = (me + i) % total_devices
        sqcopy(e, me).wait_send()
        sqcopy(e, e).wait_recv()
        return 0

    lax.fori_loop(1, total_devices, drain, 0)
    total = jnp.sum(sq[...], axis=0)
    fac_ref[...] = 1.0 / jnp.maximum(jnp.sqrt(total / total_entries), 1.0)


def fused(nd, nt, inputs, q, k, v, do, wq, wk, wv):
    seq = q.shape[1]
    kv = k.shape[2] // HEAD_SIZE
    wide = (q.shape[2] + 2 * k.shape[2]) // kv
    rows = wq.shape[0]
    half = seq // nt
    group = nd // 2
    total_entries = float(rows * nd * kv * wide * nt)
    vm = pl.BlockSpec(memory_space=pltpu.VMEM)
    dma = pltpu.SemaphoreType.DMA
    return pl.pallas_call(
        functools.partial(kernel, nd, total_entries),
        out_shape=(
            jax.ShapeDtypeStruct(inputs.shape, BF16),
            jax.ShapeDtypeStruct(wq.shape, F32),
            jax.ShapeDtypeStruct(wk.shape, F32),
            jax.ShapeDtypeStruct(wv.shape, F32),
            jax.ShapeDtypeStruct((8, 128), F32),
        ),
        in_specs=[vm] * 8,
        out_specs=(vm,) * 5,
        scratch_shapes=[
            pltpu.VMEM((kv, group, seq, wide), BF16),
            pltpu.VMEM((group, nt, half, 2 * rows), BF16),
            pltpu.VMEM((kv, 2 * rows, wide), BF16),
            pltpu.VMEM((kv, 2 * rows, wide), F32),
            pltpu.VMEM((group // 2 * seq, 2 * rows), F32),
            pltpu.VMEM((group, nt, half, 2 * rows), BF16),
            pltpu.VMEM((group, half, 2 * rows), BF16),
            pltpu.VMEM((group, half, 2 * rows), BF16),
            pltpu.VMEM((kv, rows, wide), BF16),
            pltpu.VMEM((kv, rows, wide), BF16),
            pltpu.VMEM((nd * nt, 8, 128), F32),
            dma((group, 2)), dma((group, 2)), dma((group,)), dma((group,)),
            dma((kv,)), dma((kv,)), dma((kv,)), dma((kv,)),
            dma((2, kv)), dma((2, kv)), dma((4, kv)), dma((4, kv)),
            dma((group,)), dma((group,)), dma((group, 2)), dma((group, 2)),
            dma((kv,)), dma((kv,)), dma((nd * nt,)), dma((nd * nt,)),
        ],
        compiler_params=pltpu.CompilerParams(
            collective_id=0, has_side_effects=True, vmem_limit_bytes=60 * 1024 * 1024
        ),
    )(inputs, q, k, v, do, wq, wk, wv)


def heads_backward(query_row_set, key_rows, value_rows, cotangent_rows):
    token_length = query_row_set.shape[0]
    kv_heads = key_rows.shape[1] // HEAD_SIZE
    group_width = query_row_set.shape[1] // HEAD_SIZE // kv_heads
    scaling = 1.0 / math.sqrt(HEAD_SIZE)
    query_quad = query_row_set.reshape(token_length, kv_heads, group_width, HEAD_SIZE)
    cotangent_quad = cotangent_rows.reshape(token_length, kv_heads, group_width, HEAD_SIZE)
    key_triple = key_rows.reshape(token_length, kv_heads, HEAD_SIZE)
    value_triple = value_rows.reshape(token_length, kv_heads, HEAD_SIZE)
    block_rows = min(token_length, 512)
    key_sums = jnp.zeros((token_length, kv_heads, HEAD_SIZE), F32)
    value_sums = jnp.zeros((token_length, kv_heads, HEAD_SIZE), F32)
    query_blocks = []
    for row_start in range(0, token_length, block_rows):
        row_end = row_start + block_rows
        query_block = query_quad[row_start:row_end]
        cotangent_block = cotangent_quad[row_start:row_end]
        key_block = key_triple[:row_end]
        value_block = value_triple[:row_end]
        scores = (
            jnp.einsum("ihgd,jhd->hgij", query_block, key_block, preferred_element_type=F32)
            * scaling
        )
        query_index = row_start + lax.broadcasted_iota(jnp.int32, (block_rows, row_end), 0)
        key_index = lax.broadcasted_iota(jnp.int32, (block_rows, row_end), 1)
        scores = jnp.where(query_index >= key_index, scores, -jnp.inf)
        maximum = jnp.max(scores, axis=-1, keepdims=True)
        exponent = jnp.exp(scores - maximum)
        softmax_rows = exponent / jnp.sum(exponent, axis=-1, keepdims=True)
        softmax_reduced = softmax_rows.astype(BF16)
        grad_softmax = jnp.einsum(
            "ihgd,jhd->hgij", cotangent_block, value_block, preferred_element_type=F32
        )
        row_delta = jnp.sum(softmax_rows * grad_softmax, axis=-1, keepdims=True)
        score_gradient = (softmax_rows * (grad_softmax - row_delta) * scaling).astype(BF16)
        query_blocks.append(
            jnp.einsum(
                "hgij,jhd->ihgd", score_gradient, key_block, preferred_element_type=F32
            ).astype(BF16)
        )
        key_sums = key_sums.at[:row_end].add(
            jnp.einsum(
                "xfwo,wxfp->oxp", score_gradient, query_block, preferred_element_type=F32
            )
        )
        value_sums = value_sums.at[:row_end].add(
            jnp.einsum(
                "xfwo,wxfp->oxp",
                softmax_reduced,
                cotangent_block,
                preferred_element_type=F32,
            )
        )
    grad_query = jnp.concatenate(query_blocks, axis=0).reshape(token_length, -1)
    key_gradient = key_sums.astype(BF16).reshape(token_length, -1)
    value_gradient = value_sums.astype(BF16).reshape(token_length, -1)
    return (grad_query, key_gradient, value_gradient)


def small(nd, nt, inputs, query_states, key_states, query_weight):
    seq = query_states.shape[1]
    cols = query_states.shape[2] + 2 * key_states.shape[2]
    held = nd * seq * cols * 2 + 10 * nd * seq * query_weight.shape[0]
    return nt == 2 and nd == 16 and held < 36 * 1024 * 1024


def local(nd, nt, *args):
    inputs, q, k, v, do, wq, wk, wv, mq, mk, mv = args
    if small(nd, nt, inputs, q, k, wq):
        grad_inputs, gq, gk, gv, fac = fused(nd, nt, inputs, q, k, v, do, wq, wk, wv)
        factor = fac[0, 0]
    else:
        query_cols = wq.shape[1]
        pair_cols = wk.shape[1]
        rows = wq.shape[0]
        weights = jnp.concatenate((wq, wk, wv), axis=1)
        grads = jnp.concatenate(heads_backward(q[0], k[0], v[0], do[0]), axis=1)
        all_grads = lax.all_gather(grads, "dp", axis=0, tiled=True)
        pieces = lax.all_to_all(inputs[0], "dp", 1, 0, tiled=True)
        pieces = pieces.reshape(nd, -1, rows)
        all_inputs = lax.all_gather(pieces, "tensor", axis=1, tiled=True).reshape(-1, rows)
        summed = dot(all_inputs, all_grads, 0, 0)
        parts = dot(all_grads, weights, 1, 1).astype(BF16).reshape(nd, -1, rows)
        mine = lax.psum_scatter(parts, "tensor", scatter_dimension=1, tiled=True)
        grad_inputs = lax.all_to_all(mine.reshape(-1, rows), "dp", 0, 1, tiled=True)[None]
        total = lax.psum(jnp.sum(summed * summed), ("dp", "tensor"))
        factor = 1.0 / jnp.maximum(jnp.sqrt(total / (summed.size * nd * nt)), 1.0)
        gq = summed[:, :query_cols]
        gk = summed[:, query_cols:query_cols + pair_cols]
        gv = summed[:, query_cols + pair_cols:]
    return (
        grad_inputs,
        0.9 * mq + factor * gq,
        0.9 * mk + factor * gk,
        0.9 * mv + factor * gv,
    )


def solution(mesh):
    nd, nt = mesh.shape["dp"], mesh.shape["tensor"]
    saved = P("dp", None, "tensor")
    tokens = P("dp", "tensor", None)
    weight = P("dp", "tensor")
    return jax.shard_map(
        functools.partial(local, nd, nt),
        mesh=mesh,
        in_specs=(tokens,) + (saved,) * 4 + (weight,) * 6,
        out_specs=(tokens,) + (weight,) * 3,
        check_vma=False,
    )
```

time: 174 us -> 176 us (1.011)
  no operation moved by 1% of the time
where the time goes in v1:
time: 176 us
  Pallas kernels  167 us (95%)
  other arithmetic  5.5 us (3%)
  local copies, waits for them, and re-layouts  2.18 us (1%)
    pallas_call x1, Pallas kernels, fused(): pl.pallas_call(functools.partial(kernel, nd, total_entries), out_shape=(j...  167 us

profile of v1, /device:TPU:0, one launch (start us, length us, event | category | flops | bytes accessed | tf_op | source)
XLA Modules:
  0.0 175.7 jit_solution(13845973104975758815)
XLA Ops:
  0.6 0.0 copy-start.3
  0.6 0.0 copy-start.4
  0.7 167.3 %shard_map.138 = (bf16[1,128,4096]{2,1,0:T(8,128)(2,1)}, f32[256,1536]{1,0:T(8,128)}, f32[256,512]{1,0:T(8,128)}, f32[256,512]{1,0:T(8,128)}, f32[8,128]{1,0:T(8,128)}) custom-call(bf16[1,128,4096]{2,1,0:T(8,128)(2,1)} %x_ref.1, bf16[1,256,1536]{2,1,0:T(8,128)(2,1)} %q_ref.1, bf16[1,256,512]{2,1,0:T(8,128)(2,1)} %k_ref.1, bf16[1,256,512]{2,1,0:T(8,128)(2,1)} %v_ref.1, ...), custom_call_target="tpu_custom_call" | custom-call | tf_op jit(solution)/shard_map/pallas_call | solution.py:342
  168.0 1.2 slice.3
  169.2 0.0 copy-done.3
  169.2 0.0 copy-done.4
  169.2 0.0 copy-start
  169.2 0.0 copy-start.1
  169.2 3.4 %multiply_add_fusion.1 = (f32[256,512]{1,0:T(8,128)}, f32[256,512]{1,0:T(8,128)}) fusion(f32[256,512]{1,0:T(8,128)} %get-tuple-element.13, f32[256,512]{1,0:T(8,128)S(1)} %copy-done.3, f32[]{:T(128)} %bitcast, f32[256,512]{1,0:T(8,128)} %get-tuple-element.12, f32[256,512]{1,0:T(8,128)S(1)} %copy-done.4), kind=kLoop, calls=%fused_computation.1 | loop fusion | flops 786432 | bytes 3145732 | tf_op jit(solution)/shard_map/add | solution.py:471
  172.5 0.0 copy-done
  172.5 0.0 copy-done.1
  172.5 0.0 copy-start.2
  172.5 2.1 %multiply_add_fusion = f32[256,1536]{1,0:T(8,128)} fusion(f32[256,1536]{1,0:T(8,128)S(1)} %copy-done.1, f32[256,1536]{1,0:T(8,128)S(1)} %copy-done, f32[]{:T(128)} %bitcast), kind=kLoop, calls=%fused_computation | loop fusion | flops 1179648 | bytes 4718596 | tf_op jit(solution)/shard_map/add | solution.py:469
  174.7 0.0 copy-done.2
  174.7 1.0 copy.16
Async XLA Ops:
  0.6 168.5 %copy-start.3 = (f32[256,512]{1,0:T(8,128)S(1)}, f32[256,512]{1,0:T(8,128)}, u32[]{:S(2)}) copy-start(f32[256,512]{1,0:T(8,128)} %param.21) | copy-start | bytes 1572868
  0.6 168.5 %copy-start.4 = (f32[256,512]{1,0:T(8,128)S(1)}, f32[256,512]{1,0:T(8,128)}, u32[]{:S(2)}) copy-start(f32[256,512]{1,0:T(8,128)} %param.20) | copy-start | bytes 1572868
  169.2 3.4 %copy-start = (f32[256,1536]{1,0:T(8,128)S(1)}, f32[256,1536]{1,0:T(8,128)}, u32[]{:S(2)}) copy-start(f32[256,1536]{1,0:T(8,128)} %param.19) | copy-start | bytes 4718596
  169.2 3.4 %copy-start.1 = (f32[256,1536]{1,0:T(8,128)S(1)}, f32[256,1536]{1,0:T(8,128)}, u32[]{:S(2)}) copy-start(f32[256,1536]{1,0:T(8,128)} %get-tuple-element.11) | copy-start | bytes 4718596
  172.5 2.2 %copy-start.2 = (bf16[1,128,4096]{2,1,0:T(8,128)(2,1)S(1)}, bf16[1,128,4096]{2,1,0:T(8,128)(2,1)}, u32[]{:S(2)}) copy-start(bf16[1,128,4096]{2,1,0:T(8,128)(2,1)} %get-tuple-element.20) | copy-start | bytes 3145732

commit v2 on v1

--- a/solution.py
+++ b/solution.py
@@ -12,7 +12,7 @@
 MESH = pl.DeviceIdType.MESH
 F32 = jnp.float32
 BF16 = jnp.bfloat16
-W_FIRST = 1
+SPLIT = 2
 
 
 def dot(a, b, ca, cb):
@@ -23,18 +23,19 @@
     nd, total_entries,
     x_ref, q_ref, k_ref, v_ref, do_ref, wq_ref, wk_ref, wv_ref,
     dx_ref, dwq_ref, dwk_ref, dwv_ref, fac_ref,
-    g_all, x_all, w_cat, acc, part, p_buf, y_buf, d_buf, ws, wr, sq,
-    xs_s, xs_r, xy_s, xy_r, w_s, w_r, col_s, col_r, xn_s, xn_r, dd_s, dd_r,
+    g_all, x_all, w_cat, acc, part, fpart, p_buf, y_buf, d_buf, ws, wr, sq,
+    xs_s, xs_r, xy_s, xy_r, w_s, w_r, col_s, col_r, re_s, re_r, fd_s, fd_r, xn_s, xn_r, dd_s, dd_r,
     py_s, py_r, dx_s, dx_r, dw_s, dw_r, sq_s, sq_r,
 ):
     kv = g_all.shape[0]
     group = g_all.shape[1]
-    seq = g_all.shape[2]
-    wide = g_all.shape[3]
+    half = g_all.shape[3]
+    seq = 2 * half
+    wide = g_all.shape[4]
     grp = q_ref.shape[2] // k_ref.shape[2]
     gq = grp * HEAD_SIZE
     rows = wq_ref.shape[0]
-    half = seq // 2
+    sub = half // SPLIT
     near = group // 2
     nz = nd // 4
     d = lax.axis_index("dp")
@@ -101,27 +102,41 @@
             w_cat.at[j, 0:rows], w_cat.at[j, rows:2 * rows], w_s.at[j], w_r.at[j], to(far, t)
         )
 
-    def colcopy(j):
-        return rcopy(g_all.at[j, 0], g_all.at[j, 4], col_s.at[j], col_r.at[j], to(member(4), t))
-
-    def xncopy(i, j):
-        return rcopy(
-            g_all.at[j, 4 * i], g_all.at[j, 4 * i + 2], xn_s.at[i, j], xn_r.at[i, j], to(member(2), t)
-        )
+    def piece(j, r, h):
+        return g_all.at[j, r, :, pl.ds(pl.multiple_of(h * sub, sub), sub)]
+
+    def colcopy(h, j):
+        return rcopy(
+            piece(j, 0, h), piece(j, 4, h), col_s.at[h, j], col_r.at[h, j], to(member(4), t)
+        )
+
+    def relay(h, j):
+        return rcopy(
+            piece(j, 4, h), piece(j, 6, h), re_s.at[h, j], re_r.at[h, j], to(member(2), t)
+        )
+
+    def fardd(i, h, j):
+        return rcopy(
+            piece(j, 4 + 2 * i, h), piece(j, 5 + 2 * i, h),
+            fd_s.at[i, h, j], fd_r.at[i, h, j], to(member(1), t),
+        )
+
+    def xncopy(j):
+        return rcopy(g_all.at[j, 0], g_all.at[j, 2], xn_s.at[j], xn_r.at[j], to(member(2), t))
 
     def ddcopy(i, j):
         return rcopy(
             g_all.at[j, 2 * i], g_all.at[j, 2 * i + 1], dd_s.at[i, j], dd_r.at[i, j], to(member(1), t)
         )
 
+    for j in range(kv):
+        wcopy(j).start()
     for r in (4, 5, 6, 7, 2, 3, 1):
         for f in range(2):
             xcopy(r, f).start()
     for f, e in ((0, d), (1, far)):
         x_all[0, t, :, f * rows:(f + 1) * rows] = x_ref[0, :, columns(e)]
     xfwd(0).start()
-    for j in range(W_FIRST):
-        wcopy(j).start()
 
     scaling = 1.0 / math.sqrt(HEAD_SIZE)
 
@@ -143,19 +158,22 @@
             gs = dot(oo, vv, 1, 1)
             delta = jnp.sum(soft * gs, axis=-1, keepdims=True)
             ds = (soft * (gs - delta) * scaling).astype(BF16)
-            g_all[j, 0, :, g * HEAD_SIZE:(g + 1) * HEAD_SIZE] = dot(ds, kk, 1, 0).astype(BF16)
+            g_all[j, 0, :, :, g * HEAD_SIZE:(g + 1) * HEAD_SIZE] = (
+                dot(ds, kk, 1, 0).astype(BF16).reshape(2, half, HEAD_SIZE)
+            )
             dk = dk + dot(ds, qq, 0, 0)
             dv = dv + dot(soft.astype(BF16), oo, 0, 0)
-        g_all[j, 0, :, gq:gq + HEAD_SIZE] = dk.astype(BF16)
-        g_all[j, 0, :, gq + HEAD_SIZE:wide] = dv.astype(BF16)
-        colcopy(j).start()
-        xncopy(0, j).start()
+        g_all[j, 0, :, :, gq:gq + HEAD_SIZE] = dk.astype(BF16).reshape(2, half, HEAD_SIZE)
+        g_all[j, 0, :, :, gq + HEAD_SIZE:wide] = dv.astype(BF16).reshape(2, half, HEAD_SIZE)
+        colcopy(0, j).start()
+        xncopy(j).start()
         ddcopy(0, j).start()
         return 0
 
     lax.fori_loop(0, kv, attention, 0)
-    for j in range(W_FIRST, kv):
-        wcopy(j).start()
+    for h in range(1, SPLIT):
+        for j in range(kv):
+            colcopy(h, j).start()
 
     def xready(r):
         for f in range(2):
@@ -165,116 +183,140 @@
     for r in range(1, group):
         xready(r)
 
-    def neighbours(j, _):
-        xncopy(0, j).wait_recv()
-        ddcopy(1, j).start()
-        ddcopy(0, j).wait_recv()
-        return 0
-
-    lax.fori_loop(0, kv, neighbours, 0)
     for r in range(group):
         xfwd_wait(r)
 
-    def near_weights(j, _):
-        ddcopy(1, j).wait_recv()
-        acc[j] = dot(x_all[0:near].reshape(near * seq, 2 * rows), g_all[j, 0:near].reshape(near * seq, wide), 0, 0)
-        return 0
-
-    lax.fori_loop(0, kv, near_weights, 0)
-
-    def partial(j, lo):
-        gs = g_all[j, lo:lo + near].reshape(near * seq, wide)
-        return dot(gs, w_cat[j], 1, 1)
-
-    def near_inputs(j, _):
-        wcopy(j).wait_recv()
-
-        @pl.when(j == 0)
-        def _():
-            part[...] = partial(j, 0)
-
-        @pl.when(j > 0)
-        def _():
-            part[...] += partial(j, 0)
-
-        return 0
-
-    lax.fori_loop(0, kv, near_inputs, 0)
-
-    def pcopy(r):
-        return rcopy(p_buf.at[r, 1 - t], y_buf.at[r], py_s.at[r], py_r.at[r], to(d, 1 - t))
-
-    def exchange(lo):
-        for r in range(near):
-            p_buf[lo + r] = part[r * seq:(r + 1) * seq].astype(BF16).reshape(2, half, 2 * rows)
-            pcopy(lo + r).start()
-
-    exchange(0)
-
-    def dxcopy(r, f):
-        e = d if f == 0 else far
-        return rcopy(
-            d_buf.at[r, :, f * rows:(f + 1) * rows], dx_ref.at[0, :, columns(e)],
-            dx_s.at[r, f], dx_r.at[r, f], to(member(r), t),
-        )
-
-    def dxwait(r, f):
-        e = member(r)
-        e = e if f == 0 else other_half(e)
-        rcopy(
-            d_buf.at[r, :, f * rows:(f + 1) * rows], dx_ref.at[0, :, columns(e)],
-            dx_s.at[r, f], dx_r.at[r, f], to(member(r), t),
-        ).wait_recv()
-
-    def finish(r):
-        pcopy(r).wait_recv()
-        total = (p_buf[r, t].astype(F32) + y_buf[r].astype(F32)).astype(BF16)
+    def pcopy(r, h):
+        span = pl.ds(pl.multiple_of(h * sub, sub), sub)
+        return rcopy(
+            p_buf.at[r, 1 - t, span], y_buf.at[r, span], py_s.at[r, h], py_r.at[r, h], to(d, 1 - t)
+        )
+
+    def dxcopy(r, f, h, e):
+        span = pl.ds(pl.multiple_of(h * sub, sub), sub)
+        return rcopy(
+            d_buf.at[r, span, f * rows:(f + 1) * rows], dx_ref.at[0, span, columns(e)],
+            dx_s.at[r, f, h], dx_r.at[r, f, h], to(member(r), t),
+        )
+
+    def finish(r, h):
+        span = pl.ds(pl.multiple_of(h * sub, sub), sub)
+        pcopy(r, h).wait_recv()
+        total = (p_buf[r, t, span].astype(F32) + y_buf[r, span].astype(F32)).astype(BF16)
         if r == 0:
             for f, e in ((0, d), (1, far)):
-                dx_ref[0, :, columns(e)] = total[:, f * rows:(f + 1) * rows]
+                dx_ref[0, span, columns(e)] = total[:, f * rows:(f + 1) * rows]
         else:
-            d_buf[r] = total
-            for f in range(2):
-                dxcopy(r, f).start()
+            d_buf[r, span] = total
+            for f, e in ((0, d), (1, far)):
+                dxcopy(r, f, h, e).start()
 
     def dwcopy(j):
         return rcopy(ws.at[j], wr.at[j], dw_s.at[j], dw_r.at[j], to(far, t))
 
-    def distant(j, _):
-        colcopy(j).wait_recv()
-        xncopy(1, j).start()
-        ddcopy(2, j).start()
+    def receive(i):
+        h = i // kv
+        j = i % kv
+        colcopy(h, j).wait_recv()
+        relay(h, j).start()
+        fardd(0, h, j).start()
+
+        @pl.when(h == 0)
+        def _():
+            xncopy(j).wait_recv()
+            ddcopy(1, j).start()
+
+    def close(j):
+        ddcopy(0, j).wait_recv()
+        ddcopy(1, j).wait_recv()
+        wcopy(j).wait_recv()
+        gs = g_all[j, 0:near].reshape(near * seq, wide)
+        acc[j] = dot(x_all[0:near].reshape(near * seq, 2 * rows), gs, 0, 0)
+        new = dot(gs, w_cat[j], 1, 1)
 
         @pl.when(j == 0)
         def _():
+            part[...] = new
+
+        @pl.when(j > 0)
+        def _():
+            part[...] += new
+
+    def distant(i):
+        h = i // kv
+        j = i % kv
+        span = pl.ds(pl.multiple_of(h * sub, sub), sub)
+        relay(h, j).wait_recv()
+        fardd(1, h, j).start()
+
+        @pl.when(h == 0)
+        def _():
+            close(j)
+
+        fardd(0, h, j).wait_recv()
+        fardd(1, h, j).wait_recv()
+        gs = g_all[j, near:group, :, span].reshape(near * 2 * sub, wide)
+        acc[j] += dot(x_all[near:group, :, span].reshape(near * 2 * sub, 2 * rows), gs, 0, 0)
+
+        @pl.when(h == SPLIT - 1)
+        def _():
+            ws[j] = acc[j, rows:2 * rows].astype(BF16)
+            dwcopy(j).start()
+
+        new = dot(gs, w_cat[j], 1, 1)
+
+        @pl.when(j == 0)
+        def _():
+            fpart[...] = new
+
+        @pl.when(j > 0)
+        def _():
+            fpart[...] += new
+
+        @pl.when(j == kv - 1)
+        def _():
+            for r in range(near, group):
+                lo = (r - near) * 2 * sub
+                p_buf[r, :, span] = (
+                    fpart[lo:lo + 2 * sub].astype(BF16).reshape(2, sub, 2 * rows)
+                )
+                pcopy(r, h).start()
+
+        @pl.when(i == kv - 1)
+        def _():
             for r in range(near):
-                finish(r)
-
-        xncopy(1, j).wait_recv()
-        ddcopy(3, j).start()
-        ddcopy(2, j).wait_recv()
-        ddcopy(3, j).wait_recv()
-        acc[j] += dot(
-            x_all[near:group].reshape(near * seq, 2 * rows),
-            g_all[j, near:group].reshape(near * seq, wide), 0, 0,
-        )
-        ws[j] = acc[j, rows:2 * rows].astype(BF16)
-        dwcopy(j).start()
-
-        @pl.when(j == 0)
-        def _():
-            part[...] = partial(j, near)
-
-        @pl.when(j > 0)
-        def _():
-            part[...] += partial(j, near)
+                p_buf[r] = part[r * seq:(r + 1) * seq].astype(BF16).reshape(2, half, 2 * rows)
+                for k in range(SPLIT):
+                    pcopy(r, k).start()
+
+    steps = SPLIT * kv
+
+    def step(i, _):
+        @pl.when(i < steps)
+        def _():
+            receive(i)
+
+        @pl.when(i > 0)
+        def _():
+            distant(i - 1)
+
+        @pl.when(i == kv + 1)
+        def _():
+            for r in range(near, group):
+                finish(r, 0)
+
+        @pl.when(i == kv + 2)
+        def _():
+            for r in range(near):
+                for k in range(SPLIT):
+                    finish(r, k)
 
         return 0
 
-    lax.fori_loop(0, kv, distant, 0)
-    exchange(near)
-    for r in range(near, group):
-        finish(r)
+    lax.fori_loop(0, steps + 1, step, 0)
+    for h in range(1, SPLIT):
+        for r in range(near, group):
+            finish(r, h)
 
     squares = jnp.zeros((1, 1), F32)
     for j in range(kv):
@@ -298,22 +340,28 @@
         dwv_ref[:, j * HEAD_SIZE:(j + 1) * HEAD_SIZE] = acc[j, 0:rows, gq + HEAD_SIZE:wide]
 
     for r in range(1, group):
+        e = member(r)
         for f in range(2):
             xcopy(r, f).wait_send()
-            dxcopy(r, f).wait_send()
-            dxwait(r, f)
+            for h in range(SPLIT):
+                dxcopy(r, f, h, d).wait_send()
+                dxcopy(r, f, h, e if f == 0 else other_half(e)).wait_recv()
     for r in range(group):
         xfwd(r).wait_send()
-        pcopy(r).wait_send()
+        for h in range(SPLIT):
+            pcopy(r, h).wait_send()
 
     def drain_g(j, _):
         wcopy(j).wait_send()
         dwcopy(j).wait_send()
-        colcopy(j).wait_send()
+        xncopy(j).wait_send()
         for i in range(2):
-            xncopy(i, j).wait_send()
-        for i in range(4):
             ddcopy(i, j).wait_send()
+        for h in range(SPLIT):
+            colcopy(h, j).wait_send()
+            relay(h, j).wait_send()
+            for i in range(2):
+                fardd(i, h, j).wait_send()
         return 0
 
     lax.fori_loop(0, kv, drain_g, 0)
@@ -351,11 +399,12 @@
         in_specs=[vm] * 8,
         out_specs=(vm,) * 5,
         scratch_shapes=[
-            pltpu.VMEM((kv, group, seq, wide), BF16),
+            pltpu.VMEM((kv, group, nt, half, wide), BF16),
             pltpu.VMEM((group, nt, half, 2 * rows), BF16),
             pltpu.VMEM((kv, 2 * rows, wide), BF16),
             pltpu.VMEM((kv, 2 * rows, wide), F32),
             pltpu.VMEM((group // 2 * seq, 2 * rows), F32),
+            pltpu.VMEM((group // 2 * seq // SPLIT, 2 * rows), F32),
             pltpu.VMEM((group, nt, half, 2 * rows), BF16),
             pltpu.VMEM((group, half, 2 * rows), BF16),
             pltpu.VMEM((group, half, 2 * rows), BF16),
@@ -363,9 +412,10 @@
             pltpu.VMEM((kv, rows, wide), BF16),
             pltpu.VMEM((nd * nt, 8, 128), F32),
             dma((group, 2)), dma((group, 2)), dma((group,)), dma((group,)),
-            dma((kv,)), dma((kv,)), dma((kv,)), dma((kv,)),
-            dma((2, kv)), dma((2, kv)), dma((4, kv)), dma((4, kv)),
-            dma((group,)), dma((group,)), dma((group, 2)), dma((group, 2)),
+            dma((kv,)), dma((kv,)), dma((SPLIT, kv)), dma((SPLIT, kv)),
+            dma((SPLIT, kv)), dma((SPLIT, kv)), dma((2, SPLIT, kv)), dma((2, SPLIT, kv)),
+            dma((kv,)), dma((kv,)), dma((2, kv)), dma((2, kv)),
+            dma((group, SPLIT)), dma((group, SPLIT)), dma((group, 2, SPLIT)), dma((group, 2, SPLIT)),
             dma((kv,)), dma((kv,)), dma((nd * nt,)), dma((nd * nt,)),
         ],
         compiler_params=pltpu.CompilerParams(

time: 176 us -> 144 us (0.82)
  Pallas kernels: 167 us -> 135 us
    pallas_call x1, Pallas kernels: 167 us -> 135 us  [fused(): pl.pallas_call(functools.partial(kernel, nd, total_entries), out_shape=(j...]
where the time goes in v2:
time: 144 us
  Pallas kernels  135 us (94%)
  other arithmetic  5.5 us (4%)
  local copies, waits for them, and re-layouts  2.18 us (2%)
    pallas_call x1, Pallas kernels, fused(): pl.pallas_call(functools.partial(kernel, nd, total_entries), out_shape=(j...  135 us
    add x1, other arithmetic, local(): 0.9 * mv + factor * gv  3.35 us

profile of v2, /device:TPU:0, one launch (start us, length us, event | category | flops | bytes accessed | tf_op | source)
XLA Modules:
  0.0 143.8 jit_solution(18191939030390700828)
XLA Ops:
  0.6 0.0 copy-start.3
  0.6 0.0 copy-start.4
  0.7 135.4 %shard_map.138 = (bf16[1,128,4096]{2,1,0:T(8,128)(2,1)}, f32[256,1536]{1,0:T(8,128)}, f32[256,512]{1,0:T(8,128)}, f32[256,512]{1,0:T(8,128)}, f32[8,128]{1,0:T(8,128)}) custom-call(bf16[1,128,4096]{2,1,0:T(8,128)(2,1)} %x_ref.1, bf16[1,256,1536]{2,1,0:T(8,128)(2,1)} %q_ref.1, bf16[1,256,512]{2,1,0:T(8,128)(2,1)} %k_ref.1, bf16[1,256,512]{2,1,0:T(8,128)(2,1)} %v_ref.1, ...), custom_call_target="tpu_custom_call" | custom-call | tf_op jit(solution)/shard_map/pallas_call | solution.py:390
  136.1 1.2 slice.3
  137.3 0.0 copy-done.3
  137.3 0.0 copy-done.4
  137.3 0.0 copy-start
  137.3 0.0 copy-start.1
  137.3 3.4 %multiply_add_fusion.1 = (f32[256,512]{1,0:T(8,128)}, f32[256,512]{1,0:T(8,128)}) fusion(f32[256,512]{1,0:T(8,128)} %get-tuple-element.13, f32[256,512]{1,0:T(8,128)S(1)} %copy-done.3, f32[]{:T(128)} %bitcast, f32[256,512]{1,0:T(8,128)} %get-tuple-element.12, f32[256,512]{1,0:T(8,128)S(1)} %copy-done.4), kind=kLoop, calls=%fused_computation.1 | loop fusion | flops 786432 | bytes 3145732 | tf_op jit(solution)/shard_map/add | solution.py:521
  140.7 0.0 copy-done
  140.7 0.0 copy-done.1
  140.7 0.0 copy-start.2
  140.7 2.1 %multiply_add_fusion = f32[256,1536]{1,0:T(8,128)} fusion(f32[256,1536]{1,0:T(8,128)S(1)} %copy-done.1, f32[256,1536]{1,0:T(8,128)S(1)} %copy-done, f32[]{:T(128)} %bitcast), kind=kLoop, calls=%fused_computation | loop fusion | flops 1179648 | bytes 4718596 | tf_op jit(solution)/shard_map/add | solution.py:519
  142.8 0.0 copy-done.2
  142.8 1.0 copy.16
Async XLA Ops:
  0.6 136.7 %copy-start.3 = (f32[256,512]{1,0:T(8,128)S(1)}, f32[256,512]{1,0:T(8,128)}, u32[]{:S(2)}) copy-start(f32[256,512]{1,0:T(8,128)} %param.21) | copy-start | bytes 1572868
  0.6 136.7 %copy-start.4 = (f32[256,512]{1,0:T(8,128)S(1)}, f32[256,512]{1,0:T(8,128)}, u32[]{:S(2)}) copy-start(f32[256,512]{1,0:T(8,128)} %param.20) | copy-start | bytes 1572868
  137.3 3.4 %copy-start = (f32[256,1536]{1,0:T(8,128)S(1)}, f32[256,1536]{1,0:T(8,128)}, u32[]{:S(2)}) copy-start(f32[256,1536]{1,0:T(8,128)} %param.19) | copy-start | bytes 4718596
  137.3 3.4 %copy-start.1 = (f32[256,1536]{1,0:T(8,128)S(1)}, f32[256,1536]{1,0:T(8,128)}, u32[]{:S(2)}) copy-start(f32[256,1536]{1,0:T(8,128)} %get-tuple-element.11) | copy-start | bytes 4718596
  140.7 2.2 %copy-start.2 = (bf16[1,128,4096]{2,1,0:T(8,128)(2,1)S(1)}, bf16[1,128,4096]{2,1,0:T(8,128)(2,1)}, u32[]{:S(2)}) copy-start(bf16[1,128,4096]{2,1,0:T(8,128)(2,1)} %get-tuple-element.20) | copy-start | bytes 3145732

commit v3 on v2

--- a/solution.py
+++ b/solution.py
@@ -21,11 +21,12 @@
 
 def kernel(
     nd, total_entries,
-    x_ref, q_ref, k_ref, v_ref, do_ref, wq_ref, wk_ref, wv_ref,
-    dx_ref, dwq_ref, dwk_ref, dwv_ref, fac_ref,
-    g_all, x_all, w_cat, acc, part, fpart, p_buf, y_buf, d_buf, ws, wr, sq,
+    x_in, q_in, k_in, v_in, do_in, wq_ref, wk_ref, wv_ref, mq_ref, mk_ref, mv_ref,
+    dx_out, vq_out, vk_out, vv_out,
+    g_all, x_all, w_cat, acc, part, fpart, p_buf, y_buf, d_buf, ws, wr, sq, mq, mk, mv,
+    x_ref, q_ref, k_ref, v_ref, do_ref, dx_ref,
     xs_s, xs_r, xy_s, xy_r, w_s, w_r, col_s, col_r, re_s, re_r, fd_s, fd_r, xn_s, xn_r, dd_s, dd_r,
-    py_s, py_r, dx_s, dx_r, dw_s, dw_r, sq_s, sq_r,
+    py_s, py_r, dx_s, dx_r, dw_s, dw_r, sq_s, sq_r, m_s, in_s, win_s, dxo_s, vo_s,
 ):
     kv = g_all.shape[0]
     group = g_all.shape[1]
@@ -75,12 +76,33 @@
         return 0
 
     lax.fori_loop(1, total_devices, sig, 0)
-
+    pieces = []
     for j in range(kv):
-        w_cat[j, 0:rows, 0:gq] = wq_ref[:, j * gq:(j + 1) * gq]
-        w_cat[j, 0:rows, gq:gq + HEAD_SIZE] = wk_ref[:, j * HEAD_SIZE:(j + 1) * HEAD_SIZE]
-        w_cat[j, 0:rows, gq + HEAD_SIZE:wide] = wv_ref[:, j * HEAD_SIZE:(j + 1) * HEAD_SIZE]
-
+        cq = slice(j * gq, (j + 1) * gq)
+        ck = slice(j * HEAD_SIZE, (j + 1) * HEAD_SIZE)
+        for i, (src, cut, lo, hi) in enumerate((
+            (wq_ref, cq, 0, gq), (wk_ref, ck, gq, gq + HEAD_SIZE), (wv_ref, ck, gq + HEAD_SIZE, wide)
+        )):
+            pieces.append(
+                pltpu.make_async_copy(src.at[:, cut], w_cat.at[j, 0:rows, lo:hi], win_s.at[j, i])
+            )
+    loads = [
+        pltpu.make_async_copy(src, dst, in_s.at[i])
+        for i, (src, dst) in enumerate(
+            ((x_in, x_ref), (k_in, k_ref), (q_in, q_ref), (v_in, v_ref), (do_in, do_ref))
+        )
+    ]
+    for copy in (loads[0], *pieces, *loads[1:]):
+        copy.start()
+    momentum = [
+        pltpu.make_async_copy(src, dst, m_s.at[i])
+        for i, (src, dst) in enumerate(((mq_ref, mq), (mk_ref, mk), (mv_ref, mv)))
+    ]
+    for copy in momentum:
+        copy.start()
+
+    for copy in (loads[0], *pieces):
+        copy.wait()
     pl.semaphore_wait(bar, total_devices - 1)
 
     def xcopy(r, f):
@@ -138,6 +160,8 @@
         x_all[0, t, :, f * rows:(f + 1) * rows] = x_ref[0, :, columns(e)]
     xfwd(0).start()
 
+    for copy in loads[1:]:
+        copy.wait()
     scaling = 1.0 / math.sqrt(HEAD_SIZE)
 
     def attention(j, _):
@@ -300,22 +324,19 @@
         def _():
             distant(i - 1)
 
-        @pl.when(i == kv + 1)
+        @pl.when(i == steps)
         def _():
             for r in range(near, group):
                 finish(r, 0)
-
-        @pl.when(i == kv + 2)
-        def _():
-            for r in range(near):
-                for k in range(SPLIT):
-                    finish(r, k)
 
         return 0
 
     lax.fori_loop(0, steps + 1, step, 0)
     for h in range(1, SPLIT):
         for r in range(near, group):
+            finish(r, h)
+    for r in range(near):
+        for h in range(SPLIT):
             finish(r, h)
 
     squares = jnp.zeros((1, 1), F32)
@@ -324,7 +345,7 @@
         a = acc[j, 0:rows] + wr[j].astype(F32)
         acc[j, 0:rows] = a
         squares = squares + jnp.sum(a * a, keepdims=True)
-    sq[me] = jnp.broadcast_to(squares, (8, 128))
+    sq[me] = jnp.broadcast_to(squares, (1, 128))
 
     def sqcopy(e, slot):
         return rcopy(sq.at[slot], sq.at[slot], sq_s.at[e], sq_r.at[slot], to(e // 2, e % 2))
@@ -334,10 +355,6 @@
         return 0
 
     lax.fori_loop(1, total_devices, sqsend, 0)
-    for j in range(kv):
-        dwq_ref[:, j * gq:(j + 1) * gq] = acc[j, 0:rows, 0:gq]
-        dwk_ref[:, j * HEAD_SIZE:(j + 1) * HEAD_SIZE] = acc[j, 0:rows, gq:gq + HEAD_SIZE]
-        dwv_ref[:, j * HEAD_SIZE:(j + 1) * HEAD_SIZE] = acc[j, 0:rows, gq + HEAD_SIZE:wide]
 
     for r in range(1, group):
         e = member(r)
@@ -346,6 +363,8 @@
             for h in range(SPLIT):
                 dxcopy(r, f, h, d).wait_send()
                 dxcopy(r, f, h, e if f == 0 else other_half(e)).wait_recv()
+    dx_store = pltpu.make_async_copy(dx_ref, dx_out, dxo_s)
+    dx_store.start()
     for r in range(group):
         xfwd(r).wait_send()
         for h in range(SPLIT):
@@ -373,11 +392,27 @@
         return 0
 
     lax.fori_loop(1, total_devices, drain, 0)
-    total = jnp.sum(sq[...], axis=0)
-    fac_ref[...] = 1.0 / jnp.maximum(jnp.sqrt(total / total_entries), 1.0)
-
-
-def fused(nd, nt, inputs, q, k, v, do, wq, wk, wv):
+    total = jnp.sum(sq[...], axis=0)[0:1, 0:1]
+    factor = 1.0 / jnp.maximum(jnp.sqrt(total / total_entries), 1.0)
+    for copy in momentum:
+        copy.wait()
+    stores = []
+    for j in range(kv):
+        cq = slice(j * gq, (j + 1) * gq)
+        ck = slice(j * HEAD_SIZE, (j + 1) * HEAD_SIZE)
+        for i, (buf, dst, cut, lo, hi) in enumerate((
+            (mq, vq_out, cq, 0, gq),
+            (mk, vk_out, ck, gq, gq + HEAD_SIZE),
+            (mv, vv_out, ck, gq + HEAD_SIZE, wide),
+        )):
+            buf[:, cut] = 0.9 * buf[:, cut] + factor * acc[j, 0:rows, lo:hi]
+            stores.append(pltpu.make_async_copy(buf.at[:, cut], dst.at[:, cut], vo_s.at[j, i]))
+            stores[-1].start()
+    for copy in (dx_store, *stores):
+        copy.wait()
+
+
+def fused(nd, nt, inputs, q, k, v, do, wq, wk, wv, mq, mk, mv):
     seq = q.shape[1]
     kv = k.shape[2] // HEAD_SIZE
     wide = (q.shape[2] + 2 * k.shape[2]) // kv
@@ -385,7 +420,6 @@
     half = seq // nt
     group = nd // 2
     total_entries = float(rows * nd * kv * wide * nt)
-    vm = pl.BlockSpec(memory_space=pltpu.VMEM)
     dma = pltpu.SemaphoreType.DMA
     return pl.pallas_call(
         functools.partial(kernel, nd, total_entries),
@@ -394,10 +428,9 @@
             jax.ShapeDtypeStruct(wq.shape, F32),
             jax.ShapeDtypeStruct(wk.shape, F32),
             jax.ShapeDtypeStruct(wv.shape, F32),
-            jax.ShapeDtypeStruct((8, 128), F32),
         ),
-        in_specs=[vm] * 8,
-        out_specs=(vm,) * 5,
+        in_specs=[pl.BlockSpec(memory_space=pltpu.HBM)] * 11,
+        out_specs=(pl.BlockSpec(memory_space=pltpu.HBM),) * 4,
         scratch_shapes=[
             pltpu.VMEM((kv, group, nt, half, wide), BF16),
             pltpu.VMEM((group, nt, half, 2 * rows), BF16),
@@ -410,18 +443,62 @@
             pltpu.VMEM((group, half, 2 * rows), BF16),
             pltpu.VMEM((kv, rows, wide), BF16),
             pltpu.VMEM((kv, rows, wide), BF16),
-            pltpu.VMEM((nd * nt, 8, 128), F32),
+            pltpu.VMEM((nd * nt, 1, 128), F32),
+            pltpu.VMEM(mq.shape, F32),
+            pltpu.VMEM(mk.shape, F32),
+            pltpu.VMEM(mv.shape, F32),
+            pltpu.VMEM(inputs.shape, BF16),
+            pltpu.VMEM(q.shape, BF16),
+            pltpu.VMEM(k.shape, BF16),
+            pltpu.VMEM(v.shape, BF16),
+            pltpu.VMEM(do.shape, BF16),
+            pltpu.VMEM(inputs.shape, BF16),
             dma((group, 2)), dma((group, 2)), dma((group,)), dma((group,)),
             dma((kv,)), dma((kv,)), dma((SPLIT, kv)), dma((SPLIT, kv)),
             dma((SPLIT, kv)), dma((SPLIT, kv)), dma((2, SPLIT, kv)), dma((2, SPLIT, kv)),
             dma((kv,)), dma((kv,)), dma((2, kv)), dma((2, kv)),
             dma((group, SPLIT)), dma((group, SPLIT)), dma((group, 2, SPLIT)), dma((group, 2, SPLIT)),
-            dma((kv,)), dma((kv,)), dma((nd * nt,)), dma((nd * nt,)),
+            dma((kv,)), dma((kv,)), dma((nd * nt,)), dma((nd * nt,)), dma((3,)), dma((5,)), dma((kv, 3)), dma, dma((kv, 3)),
         ],
         compiler_params=pltpu.CompilerParams(
             collective_id=0, has_side_effects=True, vmem_limit_bytes=60 * 1024 * 1024
         ),
-    )(inputs, q, k, v, do, wq, wk, wv)
+    )(inputs, q, k, v, do, wq, wk, wv, mq, mk, mv)
+
+
+def pieces_of(shape):
+    axis = len(shape) - 2
+    step = shape[axis] // 2
+    return [(slice(None),) * axis + (slice(i * step, (i + 1) * step),) for i in range(2)]
+
+
+def hand_kernel(*refs):
+    ins, outs, bufs, (get_s, put_s) = refs[0:4], refs[4:8], refs[8:12], refs[12:14]
+    gets, puts = [], []
+    for i in range(4):
+        for k, cut in enumerate(pieces_of(ins[i].shape)):
+            gets.append(pltpu.make_async_copy(ins[i].at[cut], bufs[i].at[cut], get_s.at[i, k]))
+            puts.append(pltpu.make_async_copy(bufs[i].at[cut], outs[i].at[cut], put_s.at[i, k]))
+    for get in gets:
+        get.start()
+    for get, put in zip(gets, puts):
+        get.wait()
+        put.start()
+    for put in puts:
+        put.wait()
+
+
+def handed(*arrays):
+    hbm = pl.BlockSpec(memory_space=pltpu.HBM)
+    return pl.pallas_call(
+        hand_kernel,
+        out_shape=tuple(jax.ShapeDtypeStruct(a.shape, a.dtype) for a in arrays),
+        in_specs=[hbm] * 4,
+        out_specs=(hbm,) * 4,
+        scratch_shapes=[pltpu.VMEM(a.shape, a.dtype) for a in arrays]
+        + [pltpu.SemaphoreType.DMA((4, 2))] * 2,
+        compiler_params=pltpu.CompilerParams(vmem_limit_bytes=60 * 1024 * 1024),
+    )(*arrays)
 
 
 def heads_backward(query_row_set, key_rows, value_rows, cotangent_rows):
@@ -493,8 +570,7 @@
 def local(nd, nt, *args):
     inputs, q, k, v, do, wq, wk, wv, mq, mk, mv = args
     if small(nd, nt, inputs, q, k, wq):
-        grad_inputs, gq, gk, gv, fac = fused(nd, nt, inputs, q, k, v, do, wq, wk, wv)
-        factor = fac[0, 0]
+        return handed(*fused(nd, nt, *args))
     else:
         query_cols = wq.shape[1]
         pair_cols = wk.shape[1]

time: 144 us -> 138 us (0.958)
  other arithmetic: 5.5 us -> 0 us
  local copies, waits for them, and re-layouts: 2.18 us -> 0 us
  Pallas kernels: 135 us -> 137 us
    add x2 -> x0, other arithmetic: 5.5 us -> none  [the longest x1 3.35 us: local(): 0.9 * mv + factor * gv]
    pallas_call x0 -> x1, Pallas kernels: none -> 3.07 us  [handed(): pl.pallas_call(hand_kernel, out_shape=tuple((jax.ShapeDtypeStruct(a.shape...]
    pallas_call x1, Pallas kernels: 135 us -> 134 us  [fused(): pl.pallas_call(functools.partial(kernel, nd, total_entries), out_shape=(j...]
where the time goes in v3:
time: 138 us; the launch traced here: 137 us
  Pallas kernels  137 us (99%)
    pallas_call x1, Pallas kernels, fused(): pl.pallas_call(functools.partial(kernel, nd, total_entries), out_shape=(j...  134 us
    pallas_call x1, Pallas kernels, handed(): pl.pallas_call(hand_kernel, out_shape=tuple((jax.ShapeDtypeStruct(a.shape...  3.07 us

profile of v3, /device:TPU:0, one launch (start us, length us, event | category | flops | bytes accessed | tf_op | source)
XLA Modules:
  0.0 137.4 jit_solution(11838928053457976507)
XLA Ops:
  0.6 133.6 %shard_map.138 = (bf16[1,128,4096]{2,1,0:T(8,128)(2,1)}, f32[256,1536]{1,0:T(8,128)}, f32[256,512]{1,0:T(8,128)}, f32[256,512]{1,0:T(8,128)}) custom-call(bf16[1,128,4096]{2,1,0:T(8,128)(2,1)} %x_in.1, bf16[1,256,1536]{2,1,0:T(8,128)(2,1)} %q_in.1, bf16[1,256,512]{2,1,0:T(8,128)(2,1)} %k_in.1, bf16[1,256,512]{2,1,0:T(8,128)(2,1)} %v_in.1, ...), custom_call_target="tpu_custom_call" | custom-call | tf_op jit(solution)/shard_map/pallas_call | solution.py:424
  134.3 3.1 %shard_map.139 = (bf16[1,128,4096]{2,1,0:T(8,128)(2,1)}, f32[256,1536]{1,0:T(8,128)}, f32[256,512]{1,0:T(8,128)}, f32[256,512]{1,0:T(8,128)}) custom-call(bf16[1,128,4096]{2,1,0:T(8,128)(2,1)} %get-tuple-element.8.refs_0_, f32[256,1536]{1,0:T(8,128)} %get-tuple-element.9.refs_1_, f32[256,512]{1,0:T(8,128)} %get-tuple-element.10.refs_2_, ...), custom_call_target="tpu_custom_call" | custom-call | tf_op jit(solution)/shard_map/pallas_call | solution.py:493

commit v4 on v3

--- a/solution.py
+++ b/solution.py
@@ -13,6 +13,7 @@
 F32 = jnp.float32
 BF16 = jnp.bfloat16
 SPLIT = 2
+AHEAD = 4
 
 
 def dot(a, b, ca, cb):
@@ -66,6 +67,8 @@
         )
 
     far = other_half(d)
+    outer = jnp.logical_or(z == 0, z == nz - 1)
+    inner = jnp.logical_not(outer)
     me = d * 2 + t
     total_devices = nd * 2
     bar = pltpu.get_barrier_semaphore()
@@ -190,14 +193,26 @@
         g_all[j, 0, :, :, gq:gq + HEAD_SIZE] = dk.astype(BF16).reshape(2, half, HEAD_SIZE)
         g_all[j, 0, :, :, gq + HEAD_SIZE:wide] = dv.astype(BF16).reshape(2, half, HEAD_SIZE)
         colcopy(0, j).start()
-        xncopy(j).start()
+
+        @pl.when(inner)
+        def _():
+            for h in range(1, SPLIT):
+                colcopy(h, j).start()
+
+        @pl.when(jnp.logical_or(outer, j < AHEAD))
+        def _():
+            xncopy(j).start()
+
         ddcopy(0, j).start()
         return 0
 
     lax.fori_loop(0, kv, attention, 0)
-    for h in range(1, SPLIT):
-        for j in range(kv):
-            colcopy(h, j).start()
+
+    @pl.when(outer)
+    def _():
+        for h in range(1, SPLIT):
+            for j in range(kv):
+                colcopy(h, j).start()
 
     def xready(r):
         for f in range(2):
@@ -209,6 +224,8 @@
 
     for r in range(group):
         xfwd_wait(r)
+
+    steps = SPLIT * kv
 
     def pcopy(r, h):
         span = pl.ds(pl.multiple_of(h * sub, sub), sub)
@@ -238,9 +255,11 @@
     def dwcopy(j):
         return rcopy(ws.at[j], wr.at[j], dw_s.at[j], dw_r.at[j], to(far, t))
 
+    def place(i):
+        return jnp.where(outer, i // kv, i % SPLIT), jnp.where(outer, i % kv, i // SPLIT)
+
     def receive(i):
-        h = i // kv
-        j = i % kv
+        h, j = place(i)
         colcopy(h, j).wait_recv()
         relay(h, j).start()
         fardd(0, h, j).start()
@@ -249,6 +268,10 @@
         def _():
             xncopy(j).wait_recv()
             ddcopy(1, j).start()
+
+        @pl.when(jnp.logical_and(inner, jnp.logical_and(h == SPLIT - 1, j + AHEAD < kv)))
+        def _():
+            xncopy(j + AHEAD).start()
 
     def close(j):
         ddcopy(0, j).wait_recv()
@@ -267,8 +290,7 @@
             part[...] += new
 
     def distant(i):
-        h = i // kv
-        j = i % kv
+        h, j = place(i)
         span = pl.ds(pl.multiple_of(h * sub, sub), sub)
         relay(h, j).wait_recv()
         fardd(1, h, j).start()
@@ -291,29 +313,27 @@
 
         @pl.when(j == 0)
         def _():
-            fpart[...] = new
+            fpart[h] = new
 
         @pl.when(j > 0)
         def _():
-            fpart[...] += new
+            fpart[h] += new
 
         @pl.when(j == kv - 1)
         def _():
             for r in range(near, group):
                 lo = (r - near) * 2 * sub
                 p_buf[r, :, span] = (
-                    fpart[lo:lo + 2 * sub].astype(BF16).reshape(2, sub, 2 * rows)
+                    fpart[h, lo:lo + 2 * sub].astype(BF16).reshape(2, sub, 2 * rows)
                 )
                 pcopy(r, h).start()
 
-        @pl.when(i == kv - 1)
+        @pl.when(i == jnp.where(outer, kv - 1, steps - 1))
         def _():
             for r in range(near):
                 p_buf[r] = part[r * seq:(r + 1) * seq].astype(BF16).reshape(2, half, 2 * rows)
                 for k in range(SPLIT):
                     pcopy(r, k).start()
-
-    steps = SPLIT * kv
 
     def step(i, _):
         @pl.when(i < steps)
@@ -437,7 +457,7 @@
             pltpu.VMEM((kv, 2 * rows, wide), BF16),
             pltpu.VMEM((kv, 2 * rows, wide), F32),
             pltpu.VMEM((group // 2 * seq, 2 * rows), F32),
-            pltpu.VMEM((group // 2 * seq // SPLIT, 2 * rows), F32),
+            pltpu.VMEM((SPLIT, group // 2 * seq // SPLIT, 2 * rows), F32),
             pltpu.VMEM((group, nt, half, 2 * rows), BF16),
             pltpu.VMEM((group, half, 2 * rows), BF16),
             pltpu.VMEM((group, half, 2 * rows), BF16),

time: 138 us -> 131 us (0.949)
  Pallas kernels: 137 us -> 131 us
    pallas_call x1, Pallas kernels: 134 us -> 128 us  [fused(): pl.pallas_call(functools.partial(kernel, nd, total_entries), out_shape=(j...]
where the time goes in v4:
time: 131 us
  Pallas kernels  131 us (100%)
    pallas_call x1, Pallas kernels, fused(): pl.pallas_call(functools.partial(kernel, nd, total_entries), out_shape=(j...  128 us
    pallas_call x1, Pallas kernels, handed(): pl.pallas_call(hand_kernel, out_shape=tuple((jax.ShapeDtypeStruct(a.shape...  3.07 us

profile of v4, /device:TPU:0, one launch (start us, length us, event | category | flops | bytes accessed | tf_op | source)
XLA Modules:
  0.0 131.3 jit_solution(5369034300395191645)
XLA Ops:
  0.6 127.6 %shard_map.138 = (bf16[1,128,4096]{2,1,0:T(8,128)(2,1)}, f32[256,1536]{1,0:T(8,128)}, f32[256,512]{1,0:T(8,128)}, f32[256,512]{1,0:T(8,128)}) custom-call(bf16[1,128,4096]{2,1,0:T(8,128)(2,1)} %x_in.1, bf16[1,256,1536]{2,1,0:T(8,128)(2,1)} %q_in.1, bf16[1,256,512]{2,1,0:T(8,128)(2,1)} %k_in.1, bf16[1,256,512]{2,1,0:T(8,128)(2,1)} %v_in.1, ...), custom_call_target="tpu_custom_call" | custom-call | tf_op jit(solution)/shard_map/pallas_call | solution.py:444
  128.3 3.1 %shard_map.139 = (bf16[1,128,4096]{2,1,0:T(8,128)(2,1)}, f32[256,1536]{1,0:T(8,128)}, f32[256,512]{1,0:T(8,128)}, f32[256,512]{1,0:T(8,128)}) custom-call(bf16[1,128,4096]{2,1,0:T(8,128)(2,1)} %get-tuple-element.8.refs_0_, f32[256,1536]{1,0:T(8,128)} %get-tuple-element.9.refs_1_, f32[256,512]{1,0:T(8,128)} %get-tuple-element.10.refs_2_, ...), custom_call_target="tpu_custom_call" | custom-call | tf_op jit(solution)/shard_map/pallas_call | solution.py:513

commit v5 on v4

--- a/solution.py
+++ b/solution.py
@@ -13,7 +13,6 @@
 F32 = jnp.float32
 BF16 = jnp.bfloat16
 SPLIT = 2
-AHEAD = 4
 
 
 def dot(a, b, ca, cb):
@@ -73,12 +72,9 @@
     total_devices = nd * 2
     bar = pltpu.get_barrier_semaphore()
 
-    def sig(i, _):
-        e = (me + i) % total_devices
-        pl.semaphore_signal(bar, inc=1, device_id=to(e // 2, e % 2), device_id_type=MESH)
-        return 0
-
-    lax.fori_loop(1, total_devices, sig, 0)
+    for e in [member(r) for r in range(1, group)] + [far]:
+        pl.semaphore_signal(bar, inc=1, device_id=to(e, t), device_id_type=MESH)
+    pl.semaphore_signal(bar, inc=1, device_id=to(d, 1 - t), device_id_type=MESH)
     pieces = []
     for j in range(kv):
         cq = slice(j * gq, (j + 1) * gq)
@@ -106,7 +102,7 @@
 
     for copy in (loads[0], *pieces):
         copy.wait()
-    pl.semaphore_wait(bar, total_devices - 1)
+    pl.semaphore_wait(bar, group + 1)
 
     def xcopy(r, f):
         e = member(r)
@@ -194,15 +190,13 @@
         g_all[j, 0, :, :, gq + HEAD_SIZE:wide] = dv.astype(BF16).reshape(2, half, HEAD_SIZE)
         colcopy(0, j).start()
 
-        @pl.when(inner)
+        @pl.when(jnp.logical_and(inner, j % 2 == 1))
         def _():
             for h in range(1, SPLIT):
+                colcopy(h, j - 1).start()
                 colcopy(h, j).start()
 
-        @pl.when(jnp.logical_or(outer, j < AHEAD))
-        def _():
-            xncopy(j).start()
-
+        xncopy(j).start()
         ddcopy(0, j).start()
         return 0
 
@@ -256,7 +250,8 @@
         return rcopy(ws.at[j], wr.at[j], dw_s.at[j], dw_r.at[j], to(far, t))
 
     def place(i):
-        return jnp.where(outer, i // kv, i % SPLIT), jnp.where(outer, i % kv, i // SPLIT)
+        h = jnp.where(outer, i // kv, (i % (2 * SPLIT)) // 2)
+        return h, jnp.where(outer, i % kv, 2 * (i // (2 * SPLIT)) + i % 2)
 
     def receive(i):
         h, j = place(i)
@@ -264,14 +259,10 @@
         relay(h, j).start()
         fardd(0, h, j).start()
 
-        @pl.when(h == 0)
-        def _():
-            xncopy(j).wait_recv()
-            ddcopy(1, j).start()
-
-        @pl.when(jnp.logical_and(inner, jnp.logical_and(h == SPLIT - 1, j + AHEAD < kv)))
-        def _():
-            xncopy(j + AHEAD).start()
+        @pl.when(i < kv)
+        def _():
+            xncopy(i).wait_recv()
+            ddcopy(1, i).start()
 
     def close(j):
         ddcopy(0, j).wait_recv()
@@ -295,10 +286,6 @@
         relay(h, j).wait_recv()
         fardd(1, h, j).start()
 
-        @pl.when(h == 0)
-        def _():
-            close(j)
-
         fardd(0, h, j).wait_recv()
         fardd(1, h, j).wait_recv()
         gs = g_all[j, near:group, :, span].reshape(near * 2 * sub, wide)
@@ -328,23 +315,27 @@
                 )
                 pcopy(r, h).start()
 
-        @pl.when(i == jnp.where(outer, kv - 1, steps - 1))
+    def step(i, _):
+        @pl.when(i < steps)
+        def _():
+            receive(i)
+
+        @pl.when(jnp.logical_and(i > 0, i <= kv))
+        def _():
+            close(i - 1)
+
+        @pl.when(i > 0)
+        def _():
+            distant(i - 1)
+
+        @pl.when(i == kv)
         def _():
             for r in range(near):
                 p_buf[r] = part[r * seq:(r + 1) * seq].astype(BF16).reshape(2, half, 2 * rows)
-                for k in range(SPLIT):
-                    pcopy(r, k).start()
-
-    def step(i, _):
-        @pl.when(i < steps)
-        def _():
-            receive(i)
-
-        @pl.when(i > 0)
-        def _():
-            distant(i - 1)
-
-        @pl.when(i == steps)
+                for h in range(SPLIT):
+                    pcopy(r, h).start()
+
+        @pl.when(i == jnp.where(outer, kv + 2, steps))
         def _():
             for r in range(near, group):
                 finish(r, 0)
@@ -584,7 +575,8 @@
     seq = query_states.shape[1]
     cols = query_states.shape[2] + 2 * key_states.shape[2]
     held = nd * seq * cols * 2 + 10 * nd * seq * query_weight.shape[0]
-    return nt == 2 and nd == 16 and held < 36 * 1024 * 1024
+    even = key_states.shape[2] % (2 * HEAD_SIZE) == 0
+    return nt == 2 and nd == 16 and even and held < 36 * 1024 * 1024
 
 
 def local(nd, nt, *args):

time: 131 us -> 130 us (level)
  Pallas kernels: 131 us -> 129 us
    pallas_call x1, Pallas kernels: 128 us -> 126 us  [fused(): pl.pallas_call(functools.partial(kernel, nd, total_entries), out_shape=(j...]
where the time goes in v5:
time: 130 us
  Pallas kernels  129 us (99%)
    pallas_call x1, Pallas kernels, fused(): pl.pallas_call(functools.partial(kernel, nd, total_entries), out_shape=(j...  126 us
    pallas_call x1, Pallas kernels, handed(): pl.pallas_call(hand_kernel, out_shape=tuple((jax.ShapeDtypeStruct(a.shape...  3.07 us

profile of v5, /device:TPU:0, one launch (start us, length us, event | category | flops | bytes accessed | tf_op | source)
XLA Modules:
  0.0 129.9 jit_solution(4502980870701103103)
XLA Ops:
  0.6 126.2 %shard_map.138 = (bf16[1,128,4096]{2,1,0:T(8,128)(2,1)}, f32[256,1536]{1,0:T(8,128)}, f32[256,512]{1,0:T(8,128)}, f32[256,512]{1,0:T(8,128)}) custom-call(bf16[1,128,4096]{2,1,0:T(8,128)(2,1)} %x_in.1, bf16[1,256,1536]{2,1,0:T(8,128)(2,1)} %q_in.1, bf16[1,256,512]{2,1,0:T(8,128)(2,1)} %k_in.1, bf16[1,256,512]{2,1,0:T(8,128)(2,1)} %v_in.1, ...), custom_call_target="tpu_custom_call" | custom-call | tf_op jit(solution)/shard_map/pallas_call | solution.py:435
  126.8 3.1 %shard_map.139 = (bf16[1,128,4096]{2,1,0:T(8,128)(2,1)}, f32[256,1536]{1,0:T(8,128)}, f32[256,512]{1,0:T(8,128)}, f32[256,512]{1,0:T(8,128)}) custom-call(bf16[1,128,4096]{2,1,0:T(8,128)(2,1)} %get-tuple-element.8.refs_0_, f32[256,1536]{1,0:T(8,128)} %get-tuple-element.9.refs_1_, f32[256,512]{1,0:T(8,128)} %get-tuple-element.10.refs_2_, ...), custom_call_target="tpu_custom_call" | custom-call | tf_op jit(solution)/shard_map/pallas_call | solution.py:504

commit v6 on v5

--- a/solution.py
+++ b/solution.py
@@ -343,11 +343,11 @@
         return 0
 
     lax.fori_loop(0, steps + 1, step, 0)
+    for r in range(near):
+        for h in range(SPLIT):
+            finish(r, h)
     for h in range(1, SPLIT):
         for r in range(near, group):
-            finish(r, h)
-    for r in range(near):
-        for h in range(SPLIT):
             finish(r, h)
 
     squares = jnp.zeros((1, 1), F32)

time: 130 us -> 130 us (level)
  no operation moved by 1% of the time
where the time goes in v6:
time: 130 us
  Pallas kernels  129 us (99%)
    pallas_call x1, Pallas kernels, fused(): pl.pallas_call(functools.partial(kernel, nd, total_entries), out_shape=(j...  126 us
    pallas_call x1, Pallas kernels, handed(): pl.pallas_call(hand_kernel, out_shape=tuple((jax.ShapeDtypeStruct(a.shape...  3.07 us

profile of v6, /device:TPU:0, one launch (start us, length us, event | category | flops | bytes accessed | tf_op | source)
XLA Modules:
  0.0 129.9 jit_solution(17045591523151483110)
XLA Ops:
  0.6 126.2 %shard_map.138 = (bf16[1,128,4096]{2,1,0:T(8,128)(2,1)}, f32[256,1536]{1,0:T(8,128)}, f32[256,512]{1,0:T(8,128)}, f32[256,512]{1,0:T(8,128)}) custom-call(bf16[1,128,4096]{2,1,0:T(8,128)(2,1)} %x_in.1, bf16[1,256,1536]{2,1,0:T(8,128)(2,1)} %q_in.1, bf16[1,256,512]{2,1,0:T(8,128)(2,1)} %k_in.1, bf16[1,256,512]{2,1,0:T(8,128)(2,1)} %v_in.1, ...), custom_call_target="tpu_custom_call" | custom-call | tf_op jit(solution)/shard_map/pallas_call | solution.py:435
  126.8 3.1 %shard_map.139 = (bf16[1,128,4096]{2,1,0:T(8,128)(2,1)}, f32[256,1536]{1,0:T(8,128)}, f32[256,512]{1,0:T(8,128)}, f32[256,512]{1,0:T(8,128)}) custom-call(bf16[1,128,4096]{2,1,0:T(8,128)(2,1)} %get-tuple-element.8.refs_0_, f32[256,1536]{1,0:T(8,128)} %get-tuple-element.9.refs_1_, f32[256,512]{1,0:T(8,128)} %get-tuple-element.10.refs_2_, ...), custom_call_target="tpu_custom_call" | custom-call | tf_op jit(solution)/shard_map/pallas_call | solution.py:504
